TPU v7x, 128 devices: a whole 4x4x4 slice. The times are simulated.
128 devices in a mesh: node: 8 (over x, core), local: 16 (over y, z).
Axes of the slice: x: 4, y: 4, z: 4, core: 2. Of those that a mesh axis runs over, the one named last changes fastest.
Arguments:
- tokens: bfloat16 [2048, 7168], P('node', 'local'), may hold values from -6 to 6
- grad_out: bfloat16 [2048, 7168], P('node', 'local'), may hold values from -0.59765625 to 0.59765625
- gates: bfloat16 [2048, 8], P('node'), may hold values from 0.05 to 10
- routes: int32 [2048, 8], P('node'), may hold values from 0 to 31, all different within a row; in each aligned block of 256 rows (0 to 255, 256 to 511, ...) at most 80 rows name the same one
- w_gate: bfloat16 [32, 7168, 1024], P('node', 'local'), may hold values from -0.09375 to 0.09375
- w_up: bfloat16 [32, 7168, 1024], P('node', 'local'), may hold values from -0.09375 to 0.09375
- w_down: bfloat16 [32, 1024, 7168], P('node', None, 'local'), may hold values from -0.25 to 0.25
Outputs:
- grad_tokens: bfloat16 [2048, 7168], P('node', 'local')
- grad_gates: bfloat16 [2048, 8], P('node')
- grad_w_gate: bfloat16 [32, 7168, 1024], P('node', 'local')
- grad_w_up: bfloat16 [32, 7168, 1024], P('node', 'local')
- grad_w_down: bfloat16 [32, 1024, 7168], P('node', None, 'local')
- loads: float32 [32], replicated
Inputs may be any that keep to these rules, and one draw needn't show every extreme that they name: `routes`: each row names 8 different experts. Within each aligned block of 256 rows (the rows of one index of node) no expert is named by more than 80 rows, and in some blocks one expert is named by exactly 80 rows.
All inputs are finite; a program needn't handle non-finite values.
Results may differ from a plain program's by a relative error of at most 0.033.
Values may be sent and summed in bfloat16 or wider, within the bound.
A program may use at most 128 MiB of HBM per device.

v0:
```python
import jax
import jax.numpy as jnp
from jax import lax
from jax.sharding import PartitionSpec as P


def copy_for_each(array, axis):
    devices = lax.axis_size(axis)
    return lax.all_to_all(
        jnp.broadcast_to(array[None], (devices, *array.shape)), axis, 0, 0, tiled=True
    )


def over_copies(array, axis):
    return copy_for_each(array, axis).sum(axis=0)


def activation_grads(gate_pre, up_pre, back_hidden, gate_col):
    logistic = jax.nn.sigmoid(gate_pre)
    swished = gate_pre * logistic
    hidden = swished * up_pre
    products = jnp.sum(hidden * back_hidden, axis=-1)
    weight_col = gate_col.astype(jnp.float32)
    scaled = weight_col * back_hidden
    grad_up = (scaled * swished).astype(jnp.bfloat16)
    grad_gate = (scaled * up_pre * logistic * (1.0 + gate_pre * (1.0 - logistic))).astype(
        jnp.bfloat16
    )
    weighted = (weight_col * hidden).astype(jnp.bfloat16)
    return (weighted, grad_gate, grad_up, products)


def slot_tables(flat_routes, flat_gates, expert_count, capacity):
    experts_row = jnp.arange(expert_count, dtype=jnp.int32)
    onehot = (flat_routes[..., None] == experts_row).astype(jnp.int32)
    before = jnp.cumsum(onehot, axis=-2) - onehot
    slot_index = jnp.sum(before * onehot, axis=-1)
    target = flat_routes * capacity + slot_index
    weight_sum = jnp.sum(
        onehot.astype(jnp.float32) * flat_gates.astype(jnp.float32)[:, None], axis=0
    )
    return (target, weight_sum)


def on_device(tokens, grad_out, gates, routes, w_gate, w_up, w_down):
    node_count = lax.axis_size("node")
    tok_node, width_local = tokens.shape
    top_k = routes.shape[1]
    exp_node = w_gate.shape[0]
    experts = exp_node * node_count
    capacity = 5 * tok_node * top_k // (4 * experts)
    flat_routes = routes.reshape(tok_node * top_k)
    flat_gates = gates.reshape(tok_node * top_k)
    target, weight_sum = slot_tables(flat_routes, flat_gates, experts, capacity)
    summed = over_copies(weight_sum, "node")
    loads = summed * (experts / (tok_node * top_k))
    owners = jnp.arange(tok_node * top_k, dtype=jnp.int32) // top_k
    token_of = jnp.full((experts * capacity,), tok_node, jnp.int32).at[target].set(owners)
    gate_of = jnp.zeros((experts * capacity,), jnp.bfloat16).at[target].set(flat_gates)
    zero_row = jnp.zeros((1, width_local), jnp.bfloat16)
    send_tokens = jnp.concatenate([tokens, zero_row], 0)[token_of].reshape(
        node_count, exp_node, capacity, width_local
    )
    send_grads = jnp.concatenate([grad_out, zero_row], 0)[token_of].reshape(
        node_count, exp_node, capacity, width_local
    )
    send_gates = gate_of.reshape(node_count, exp_node, capacity)
    token_rows, grad_rows, gate_rows = (
        lax.all_to_all(send_tokens, "node", split_axis=0, concat_axis=0, tiled=True),
        lax.all_to_all(send_grads, "node", split_axis=0, concat_axis=0, tiled=True),
        lax.all_to_all(send_gates, "node", split_axis=0, concat_axis=0, tiled=True),
    )
    gate_pre = jnp.einsum("sjcd,jdh->sjch", token_rows, w_gate, preferred_element_type=jnp.float32)
    up_pre = jnp.einsum("sjcd,jdh->sjch", token_rows, w_up, preferred_element_type=jnp.float32)
    back_hidden = jnp.einsum(
        "sjcd,jhd->sjch", grad_rows, w_down, preferred_element_type=jnp.float32
    )
    gate_col = gate_rows[..., None]
    gate_full, up_full, back_full = (
        lax.psum(gate_pre.astype(jnp.bfloat16), "local").astype(jnp.float32),
        lax.psum(up_pre.astype(jnp.bfloat16), "local").astype(jnp.float32),
        lax.psum(back_hidden.astype(jnp.bfloat16), "local").astype(jnp.float32),
    )
    weighted, grad_gate, grad_up, products = activation_grads(
        gate_full, up_full, back_full, gate_col
    )
    grad_wg = jnp.einsum(
        "sjcd,sjch->jdh", token_rows, grad_gate, preferred_element_type=jnp.float32
    ).astype(jnp.bfloat16)
    grad_wu = jnp.einsum(
        "sjcd,sjch->jdh", token_rows, grad_up, preferred_element_type=jnp.float32
    ).astype(jnp.bfloat16)
    grad_wd = jnp.einsum(
        "sjch,sjcd->jhd", weighted, grad_rows, preferred_element_type=jnp.float32
    ).astype(jnp.bfloat16)
    input_rows = (
        jnp.einsum("sjch,jdh->sjcd", grad_gate, w_gate, preferred_element_type=jnp.float32)
        + jnp.einsum("sjch,jdh->sjcd", grad_up, w_up, preferred_element_type=jnp.float32)
    ).astype(jnp.bfloat16)
    returned_rows = lax.all_to_all(input_rows, "node", split_axis=0, concat_axis=0, tiled=True)
    returned_products = lax.all_to_all(
        products.astype(jnp.bfloat16), "node", split_axis=0, concat_axis=0, tiled=True
    )
    picked = returned_rows.reshape(experts * capacity, width_local)[target].reshape(
        tok_node, top_k, width_local
    )
    grad_tokens = jnp.sum(picked.astype(jnp.float32), axis=1).astype(jnp.bfloat16)
    grad_gates = returned_products.reshape(experts * capacity)[target].reshape(tok_node, top_k)
    return (grad_tokens, grad_gates, grad_wg, grad_wu, grad_wd, loads)


def solution(mesh):
    in_specs = (
        P("node", "local"),
        P("node", "local"),
        P("node", None),
        P("node", None),
        P("node", "local", None),
        P("node", "local", None),
        P("node", None, "local"),
    )
    out_specs = (
        P("node", "local"),
        P("node", None),
        P("node", "local", None),
        P("node", "local", None),
        P("node", None, "local"),
        P(),
    )
    return jax.shard_map(
        on_device, mesh=mesh, in_specs=in_specs, out_specs=out_specs, check_vma=False
    )
```

profile of v0, /device:TPU:1, one launch (start us, length us, event | category | flops | bytes accessed | tf_op | source)
XLA Modules:
  0.0 423.8 jit_solution(13663327641786896091)
XLA Ops:
  8.9 9.1 %reduce-window.6 = s32[32,16,128]{2,1,0:T(8,128)S(1)} reduce-window(s32[32,16,128]{2,1,0:T(8,128)S(1)} %fusion.47, s32[]{:T(128)} %constant.32.clone.1), window={size=1x1x128 pad=0_0x0_0x127_0}, to_apply=%region_0.0 | reduce-window | flops 8323072 | bytes 524292 | tf_op jit(solution)/shard_map/reduce-window
  19.1 8.1 %scatter_custom_fusion.1 = s32[2560]{0:T(1024)S(1)} fusion(s32[2048]{0:T(1024)S(1)} %bitcast.73, s32[2048]{0:T(1024)S(1)} %add_select_fusion, s32[]{:T(128)} %constant.34.clone.1), kind=kCustom, calls=%fused_computation.75 | custom fusion | bytes 10244 | tf_op jit(solution)/shard_map/scatter | solution.py:58
  28.3 8.2 %gather_fusion.1 = bf16[2560,448]{1,0:T(8,128)(2,1)} fusion(bf16[257,448]{1,0:T(8,128)(2,1)S(1)} %concatenate.7, s32[3072]{0:T(1024)S(1)} %pad_clamp_fusion), kind=kCustom, calls=%fused_computation.1 | custom fusion | bytes 4597760 | tf_op jit(solution)/shard_map/gather | solution.py:61
  36.5 5.9 %all-to-all-start.2 = ((bf16[8,4,80,448]{3,2,1,0:T(8,128)(2,1)}), bf16[8,4,80,448]{3,2,1,0:T(8,128)(2,1)S(1)}, u32[]{:S(2)}, u32[]{:S(2)}) async-start(bf16[8,4,80,448]{3,2,1,0:T(8,128)(2,1)} %bitcast.9), calls=%async_computation.2 | async-start | bytes 5242880 | tf_op jit(solution)/shard_map/all_to_all | solution.py:69
  42.6 8.2 %gather_fusion = bf16[2560,448]{1,0:T(8,128)(2,1)} fusion(bf16[257,448]{1,0:T(8,128)(2,1)S(1)} %concatenate.6, s32[3072]{0:T(1024)S(1)} %pad_clamp_fusion), kind=kCustom, calls=%fused_computation | custom fusion | bytes 4597760 | tf_op jit(solution)/shard_map/gather | solution.py:64
  50.8 23.4 %all-to-all-done.2 = bf16[8,4,80,448]{3,2,1,0:T(8,128)(2,1)S(1)} async-done(((bf16[8,4,80,448]{3,2,1,0:T(8,128)(2,1)}), bf16[8,4,80,448]{3,2,1,0:T(8,128)(2,1)S(1)}, u32[]{:S(2)}, u32[]{:S(2)}) %all-to-all-start.2) | async-done | bytes 2293792 | tf_op jit(solution)/shard_map/all_to_all | solution.py:69
  74.3 5.3 %all-to-all-start.1 = ((bf16[8,4,80,448]{3,2,1,0:T(8,128)(2,1)}), bf16[8,4,80,448]{3,2,1,0:T(8,128)(2,1)}, u32[]{:S(2)}, u32[]{:S(2)}) async-start(bf16[8,4,80,448]{3,2,1,0:T(8,128)(2,1)} %bitcast.5), calls=%async_computation.1 | async-start | bytes 5242880 | tf_op jit(solution)/shard_map/all_to_all | solution.py:70
  79.6 6.8 %convert_bitcast_fusion = bf16[8,4,80,1024]{3,2,0,1:T(8,128)(2,1)} fusion(bf16[4,448,1024]{2,1,0:T(8,128)(2,1)} %param.11, bf16[8,4,80,448]{3,2,1,0:T(8,128)(2,1)S(1)} %all-to-all-done.2), kind=kOutput, calls=%fused_computation.33 | convolution fusion | flops 2351431680 | bytes 11206656 | tf_op jit(solution)/shard_map/sjcd,jdh->sjch/dot_general | solution.py:73
  86.4 4.6 %convert_bitcast_fusion.1 = bf16[8,4,80,1024]{3,2,0,1:T(8,128)(2,1)} fusion(bf16[4,448,1024]{2,1,0:T(8,128)(2,1)S(1)} %copy-done.6, bf16[8,4,80,448]{3,2,1,0:T(8,128)(2,1)S(1)} %all-to-all-done.2), kind=kOutput, calls=%fused_computation.34 | convolution fusion | flops 2351431680 | bytes 11206656 | tf_op jit(solution)/shard_map/sjcd,jdh->sjch/dot_general | solution.py:74
  91.0 20.6 %all-to-all-done.1 = bf16[8,4,80,448]{3,2,1,0:T(8,128)(2,1)} async-done(((bf16[8,4,80,448]{3,2,1,0:T(8,128)(2,1)}), bf16[8,4,80,448]{3,2,1,0:T(8,128)(2,1)}, u32[]{:S(2)}, u32[]{:S(2)}) %all-to-all-start.1) | async-done | bytes 2293792 | tf_op jit(solution)/shard_map/all_to_all | solution.py:70
  111.5 8.0 %convert_bitcast_fusion.2 = bf16[8,4,80,1024]{3,2,0,1:T(8,128)(2,1)} fusion(bf16[4,1024,448]{1,2,0:T(8,128)(2,1)} %param.13, bf16[8,4,80,448]{3,2,1,0:T(8,128)(2,1)} %all-to-all-done.1), kind=kOutput, calls=%fused_computation.35 | convolution fusion | flops 2351431680 | bytes 11206656 | tf_op jit(solution)/shard_map/sjcd,jhd->sjch/dot_general | solution.py:75
  125.4 14.6 %scatter_custom_fusion = bf16[2560]{0:T(1024)(128)(2,1)S(1)} fusion(s32[2048]{0:T(1024)S(1)} %bitcast.75, bf16[2048]{0:T(1024)(128)(2,1)S(1)} %reshape.140, bf16[]{:T(256)} %constant.15.clone.1), kind=kCustom, calls=%fused_computation.79 | custom fusion | bytes 5122 | tf_op jit(solution)/shard_map/scatter | solution.py:59
  140.7 4.8 %all-to-all-start = ((bf16[8,4,80]{2,1,0:T(4,128)(2,1)}), bf16[8,4,80]{2,1,0:T(4,128)(2,1)S(1)}, u32[]{:S(2)}, u32[]{:S(2)}) async-start(bf16[8,4,80]{2,1,0:T(4,128)(2,1)} %reshape.97), calls=%async_computation | async-start | bytes 16384 | tf_op jit(solution)/shard_map/all_to_all | solution.py:71
  150.2 180.0 %all-reduce.5.cloned.1.call-done = (bf16[8,4,80,1024]{3,2,0,1:T(8,128)(2,1)}, bf16[8,4,80,1024]{3,2,0,1:T(8,128)(2,1)}, bf16[8,4,80,1024]{3,2,0,1:T(8,128)(2,1)}) async-done(((bf16[8,4,80,1024]{3,2,0,1:T(8,128)(2,1)}, bf16[8,4,80,1024]{3,2,0,1:T(8,128)(2,1)}, bf16[8,4,80,1024]{3,2,0,1:T(8,128)(2,1)}), (bf16[8,4,80,1024]{3,2,0,1:T(8,128)(2,1)}, bf16[8,4,80,1024]{3,2,0,1:T(8,128)(2,1)}, ...) | async-done | bytes 15728656 | tf_op jit(solution)/shard_map/psum | solution.py:81
  330.2 12.0 %fusion.2 = (bf16[8,4,80]{2,0,1:T(8,128)(2,1)S(1)}, bf16[8,4,80,1024]{3,2,0,1:T(8,128)(2,1)S(1)}, bf16[8,4,80,1024]{3,2,0,1:T(8,128)(2,1)}) fusion(bf16[8,4,80,1024]{3,2,0,1:T(8,128)(2,1)} %get-tuple-element.55, bf16[8,4,80,1024]{3,2,0,1:T(8,128)(2,1)} %get-tuple-element.54, bf16[8,4,80,1024]{3,2,0,1:T(8,128)(2,1)} %get-tuple-element.56, ...), kind=kLoop, calls=%fused_computation.15 | loop fusion | flops 52426240 | bytes 26229760 | tf_op jit(solution)/shard_map/reduce_sum | solution.py:22
  342.2 4.6 %fusion.16 = f32[4,8,80,448]{3,2,1,0:T(8,128)} fusion(bf16[8,4,80,1024]{3,2,0,1:T(8,128)(2,1)S(1)} %get-tuple-element.58, bf16[4,448,1024]{2,1,0:T(8,128)(2,1)S(1)} %copy-done.5), kind=kOutput, calls=%fused_computation.37 | convolution fusion | flops 2348810240 | bytes 13500416 | tf_op jit(solution)/shard_map/sjch,jdh->sjcd/dot_general | solution.py:97
  347.4 5.1 %all-to-all-start.4 = ((bf16[8,4,80]{2,1,0:T(4,128)(2,1)}), bf16[8,4,80]{2,1,0:T(4,128)(2,1)S(1)}, u32[]{:S(2)}, u32[]{:S(2)}) async-start(bf16[8,4,80]{2,1,0:T(4,128)(2,1)} %copy.156), calls=%async_computation.4 | async-start | bytes 16384 | tf_op jit(solution)/shard_map/all_to_all | solution.py:101
  352.5 8.1 %fusion.32 = bf16[8,4,80,448]{3,2,0,1:T(8,128)(2,1)S(1)} fusion(f32[4,8,80,448]{3,2,1,0:T(8,128)} %fusion.16, bf16[8,4,80,1024]{3,2,0,1:T(8,128)(2,1)} %get-tuple-element.59, bf16[4,448,1024]{2,1,0:T(8,128)(2,1)} %param.12), kind=kOutput, calls=%fused_computation.47 | convolution fusion | flops 2351104000 | bytes 15794176 | tf_op jit(solution)/shard_map/sjch,jdh->sjcd/dot_general | solution.py:98
  360.7 4.5 %bitcast_convert_fusion.1 = bf16[4,448,1024]{2,1,0:T(8,128)(2,1)} fusion(bf16[8,4,80,448]{3,2,1,0:T(8,128)(2,1)S(1)} %copy-done.2, bf16[8,4,80,1024]{3,2,0,1:T(8,128)(2,1)S(1)} %bitcast.68), kind=kOutput, calls=%fused_computation.25 | convolution fusion | flops 2350645248 | bytes 11206656 | tf_op jit(solution)/shard_map/sjcd,sjch->jdh/dot_general | solution.py:90
  367.0 4.8 %all-to-all-start.3 = ((bf16[8,4,80,448]{3,2,1,0:T(8,128)(2,1)}), bf16[8,4,80,448]{3,2,1,0:T(8,128)(2,1)S(1)}, u32[]{:S(2)}, u32[]{:S(2)}) async-start(bf16[8,4,80,448]{3,2,1,0:T(8,128)(2,1)} %copy.155), calls=%async_computation.3 | async-start | bytes 5242880 | tf_op jit(solution)/shard_map/all_to_all | solution.py:100
  371.8 8.2 %bitcast_convert_fusion.2 = bf16[4,448,1024]{2,1,0:T(8,128)(2,1)} fusion(bf16[8,4,80,448]{3,2,1,0:T(8,128)(2,1)} %copy-done.1, bf16[8,4,80,1024]{3,2,0,1:T(8,128)(2,1)} %copy-done), kind=kOutput, calls=%fused_computation.26 | convolution fusion | flops 2350645248 | bytes 11206656 | tf_op jit(solution)/shard_map/sjcd,sjch->jdh/dot_general | solution.py:87
  380.0 10.1 %bitcast_convert_fusion = bf16[4,1024,448]{1,2,0:T(8,128)(2,1)} fusion(bf16[8,4,80,1024]{3,2,0,1:T(8,128)(2,1)} %get-tuple-element.54, f32[8,4,80]{2,0,1:T(8,128)S(1)} %copy_convert_fusion, bf16[8,4,80,448]{3,2,1,0:T(8,128)(2,1)} %all-to-all-done.1, bf16[8,4,80,1024]{3,2,0,1:T(8,128)(2,1)} %get-tuple-element.56), kind=kOutput, calls=%fused_computation.24 | convolution fusion | flops 2374238208 | bytes 16459776 | tf_op jit(solution)/shard_map/sjch,sjcd->jhd/dot_general | solution.py:93
  390.1 13.1 %gather_fusion.3 = bf16[2048]{0:T(1024)(128)(2,1)S(1)} fusion(bf16[2560]{0:T(1024)(128)(2,1)S(1)} %reshape.102, s32[2048]{0:T(1024)S(1)} %broadcast_clamp_fusion), kind=kCustom, calls=%fused_computation.3 | custom fusion | bytes 16384 | tf_op jit(solution)/shard_map/gather | solution.py:108
  404.0 9.1 %gather_fusion.2 = bf16[2048,448]{1,0:T(8,128)(2,1)} fusion(bf16[2560,448]{1,0:T(8,128)(2,1)S(1)} %bitcast.66, s32[2048]{0:T(1024)S(1)} %broadcast_clamp_fusion), kind=kCustom, calls=%fused_computation.2 | custom fusion | bytes 3678208 | tf_op jit(solution)/shard_map/gather | solution.py:104
  (63 shorter events, 22.4 us)
Async XLA Ops:
  36.5 5.9 %copy-start.3 = (bf16[256,448]{0,1:T(8,128)(2,1)S(1)}, bf16[256,448]{0,1:T(8,128)(2,1)}, u32[]{:S(2)}) copy-start(bf16[256,448]{0,1:T(8,128)(2,1)} %param.8) | copy-start | bytes 688132
  36.5 37.7 %all-to-all-start.2 = ((bf16[8,4,80,448]{3,2,1,0:T(8,128)(2,1)}), bf16[8,4,80,448]{3,2,1,0:T(8,128)(2,1)S(1)}, u32[]{:S(2)}, u32[]{:S(2)}) async-start(bf16[8,4,80,448]{3,2,1,0:T(8,128)(2,1)} %bitcast.9), calls=%async_computation.2 | async-start | bytes 5242880 | tf_op jit(solution)/shard_map/all_to_all | solution.py:69
  74.3 12.1 %copy-start.1 = (bf16[8,4,80,448]{3,2,1,0:T(8,128)(2,1)}, bf16[8,4,80,448]{3,2,1,0:T(8,128)(2,1)S(1)}, u32[]{:S(2)}) copy-start(bf16[8,4,80,448]{3,2,1,0:T(8,128)(2,1)S(1)} %all-to-all-done.2) | copy-start | bytes 6881284
  74.3 37.2 %all-to-all-start.1 = ((bf16[8,4,80,448]{3,2,1,0:T(8,128)(2,1)}), bf16[8,4,80,448]{3,2,1,0:T(8,128)(2,1)}, u32[]{:S(2)}, u32[]{:S(2)}) async-start(bf16[8,4,80,448]{3,2,1,0:T(8,128)(2,1)} %bitcast.5), calls=%async_computation.1 | async-start | bytes 5242880 | tf_op jit(solution)/shard_map/all_to_all | solution.py:70
  79.6 250.7 %all-reduce.5.cloned.1.call-start = ((), (), s32[]{:S(2)}) async-start(), calls=%async_computation.6 | async-start | bytes 31457280 | tf_op jit(solution)/shard_map/psum | solution.py:81
  79.6 6.8 %copy-start.6 = (bf16[4,448,1024]{2,1,0:T(8,128)(2,1)S(1)}, bf16[4,448,1024]{2,1,0:T(8,128)(2,1)}, u32[]{:S(2)}) copy-start(bf16[4,448,1024]{2,1,0:T(8,128)(2,1)} %param.12) | copy-start | bytes 11010052
  119.5 0.7 copy-start.4
  121.2 19.5 %all-to-all-start.5 = ((f32[8,1,32]{2,1,0:T(1,128)}), f32[8,1,32]{2,1,0:T(1,128)S(1)}, u32[]{:S(2)}, u32[]{:S(2)}) async-start(f32[8,1,32]{2,1,0:T(1,128)} %broadcast_in_dim.11), calls=%async_computation.5 | async-start | bytes 8192 | tf_op jit(solution)/shard_map/all_to_all | solution.py:9
  140.7 9.5 %all-to-all-start = ((bf16[8,4,80]{2,1,0:T(4,128)(2,1)}), bf16[8,4,80]{2,1,0:T(4,128)(2,1)S(1)}, u32[]{:S(2)}, u32[]{:S(2)}) async-start(bf16[8,4,80]{2,1,0:T(4,128)(2,1)} %reshape.97), calls=%async_computation | async-start | bytes 16384 | tf_op jit(solution)/shard_map/all_to_all | solution.py:71
  330.2 12.0 %copy-start.5 = (bf16[4,448,1024]{2,1,0:T(8,128)(2,1)S(1)}, bf16[4,448,1024]{2,1,0:T(8,128)(2,1)}, u32[]{:S(2)}) copy-start(bf16[4,448,1024]{2,1,0:T(8,128)(2,1)} %param.11) | copy-start | bytes 11010052
  342.2 4.7 %copy-start = (bf16[8,4,80,1024]{3,2,0,1:T(8,128)(2,1)}, bf16[8,4,80,1024]{3,2,0,1:T(8,128)(2,1)S(1)}, u32[]{:S(2)}) copy-start(bf16[8,4,80,1024]{3,2,0,1:T(8,128)(2,1)S(1)} %get-tuple-element.58) | copy-start | bytes 15728644
  342.2 18.5 %slice-start = ((s8[5242880]{0:T(1024)(128)(4,1)}), s8[1048576]{0:T(1024)(128)(4,1)S(1)}, s32[]{:S(2)}) async-start(s8[5242880]{0:T(1024)(128)(4,1)} %bitcast.67), calls=%async_computation.7 | async-start | bytes 2097152
  347.4 19.5 %all-to-all-start.4 = ((bf16[8,4,80]{2,1,0:T(4,128)(2,1)}), bf16[8,4,80]{2,1,0:T(4,128)(2,1)S(1)}, u32[]{:S(2)}, u32[]{:S(2)}) async-start(bf16[8,4,80]{2,1,0:T(4,128)(2,1)} %copy.156), calls=%async_computation.4 | async-start | bytes 16384 | tf_op jit(solution)/shard_map/all_to_all | solution.py:101
  352.5 8.1 %slice-start.1 = ((s8[5242880]{0:T(1024)(128)(4,1)}), s8[4194304]{0:T(1024)(128)(4,1)S(1)}, s32[]{:S(2)}) async-start(s8[5242880]{0:T(1024)(128)(4,1)} %bitcast.67), calls=%async_computation.8 | async-start | bytes 8388608
  352.5 8.2 %copy-start.2 = (bf16[8,4,80,448]{3,2,1,0:T(8,128)(2,1)S(1)}, bf16[8,4,80,448]{3,2,1,0:T(8,128)(2,1)}, u32[]{:S(2)}) copy-start(bf16[8,4,80,448]{3,2,1,0:T(8,128)(2,1)} %copy-done.1) | copy-start | bytes 6881284
  367.0 37.0 %all-to-all-start.3 = ((bf16[8,4,80,448]{3,2,1,0:T(8,128)(2,1)}), bf16[8,4,80,448]{3,2,1,0:T(8,128)(2,1)S(1)}, u32[]{:S(2)}, u32[]{:S(2)}) async-start(bf16[8,4,80,448]{3,2,1,0:T(8,128)(2,1)} %copy.155), calls=%async_computation.3 | async-start | bytes 5242880 | tf_op jit(solution)/shard_map/all_to_all | solution.py:100
Sparse Core Ops, SparseCore 0:
  119.7 210.4 all-reduce.4
where the time goes:
time: 425 us; the launch traced here: 424 us
  waiting for transfers between devices  228 us (54%)
  local copies, waits for them, and re-layouts  70.4 us (17%)
  matrix products  55 us (13%)
  starting transfers between devices  30.1 us (7%)
  other arithmetic  25.9 us (6%)
  between operations  14.2 us (3%)
    psum x1, waiting for transfers between devices, on_device(): lax.psum(up_pre.astype(jnp.bfloat16), 'local').astype(jnp.float32)  180 us
    all_to_all x1, waiting for transfers between devices, on_device(): lax.all_to_all(send_tokens, 'node', split_axis=0, concat_axis=0, tiled=True)  23.4 us
    all_to_all x1, waiting for transfers between devices, on_device(): lax.all_to_all(send_grads, 'node', split_axis=0, concat_axis=0, tiled=True)  20.6 us
    scatter x1, local copies, waits for them, and re-layouts, on_device(): jnp.zeros((experts * capacity,), jnp.bfloat16).at[target].set(flat_gates)  14.6 us
    gather x1, local copies, waits for them, and re-layouts, on_device(): returned_products.reshape(experts * capacity)[target]  13.1 us
    reduce_sum x1, other arithmetic, activation_grads(): products = jnp.sum(hidden * back_hidden, axis=-1)  12 us
    dot_general x1, matrix products, on_device(): jnp.einsum('sjch,sjcd->jhd', weighted, grad_rows, preferred_element_type=...  10.1 us
    another operation x3, other arithmetic  9.41 us
  transfers between devices with their start and end apart: 7, of which 4 were waited for; matrix products, arithmetic and copies ran while one was open for 20% of the time, Pallas kernels for 0%

commit v1 on v0

v1 whole, which is shorter than its diff:
```python
import jax
import jax.numpy as jnp
from jax import lax
from jax.experimental import pallas as pl
from jax.experimental.pallas import tpu as pltpu
from jax.sharding import PartitionSpec as P

BF = jnp.bfloat16
F32 = jnp.float32
MESH = pl.DeviceIdType.MESH
FEAT, TOK, HID, CAPS, EXP = 448, 256, 1024, 80, 4
PAIR = 2 * TOK
ROWS = 2 * CAPS
HALF = HID // 2
BLK = 2 * FEAT + 16
CROWS = FEAT + 16
CUT = 240
ALL_EXPERTS = 32


def dot_t(a, b):
    return lax.dot_general(a, b, (((1,), (1,)), ((), ())), preferred_element_type=F32)


def dot_n(a, b):
    return jnp.dot(a, b, preferred_element_type=F32)


def add2(a, b):
    return (a.astype(F32) + b.astype(F32)).astype(BF)


def add3(a, b, c):
    return a.astype(F32) + b.astype(F32) + c.astype(F32)


def kernel(
    meta_h, tok_h, dy_h, wg_h, wu_h, wd_h,
    gt_h, gg_h, load_h, og_h, ou_h, od_h,
    wt, gat, tri, hot, slot, prt, r1a, r1b, r2a, r2b, sa, sb, r3a, r3b, r4a, r4b,
    act, dv, dr, df, acc, bk, cb, c1r, cs, c2a, c2b, c3r, gt, gg, ld,
    lsem, ssem, rsem, dsem, esem,
):
    node, local = lax.axis_index("node"), lax.axis_index("local")
    x, c = node // 2, node % 2
    y, z = local // 4, local % 4
    yp, ym, y2 = (y + 1) % 4, (y + 3) % 4, (y + 2) % 4
    zp, zm, z2 = (z + 1) % 4, (z + 3) % 4, (z + 2) % 4

    def at_x(k):
        return (((x + k) % 4) * 2 + c, local)

    def at_yz(a, b):
        return (node, a * 4 + b)

    mate = (x * 2 + 1 - c, local)
    xpd, xmd = at_x(1), at_x(3)
    ypd, ymd, zpd, zmd = at_yz(yp, z), at_yz(ym, z), at_yz(y, zp), at_yz(y, zm)
    d_z1, d_z3 = at_yz(y, z + 1 - 2 * (z % 2)), at_yz(y, 3 - z)
    d_y1, d_y3 = at_yz(y + 1 - 2 * (y % 2), z), at_yz(3 - y, z)

    def rc(src, dst, k, dev):
        return pltpu.make_async_remote_copy(
            src_ref=src, dst_ref=dst, send_sem=ssem.at[k], recv_sem=rsem.at[k],
            device_id=dev, device_id_type=MESH,
        )

    def go(copies):
        for cp in copies:
            cp.start()

    def done(copies):
        for cp in copies:
            cp.wait()

    def lane(q, base):
        return pl.ds(pl.multiple_of(base + 128 * q, 128), 128)

    lo, hi = pl.ds(0, CAPS), pl.ds(CAPS, CAPS)
    left, right = pl.ds(0, TOK), pl.ds(TOK, TOK)
    ca = pl.ds(0, HALF)

    own = [
        pltpu.make_async_copy(tok_h, gat.at[0, pl.ds(0, FEAT), left], lsem.at[0]),
        pltpu.make_async_copy(dy_h, gat.at[0, pl.ds(FEAT, FEAT), left], lsem.at[1]),
        pltpu.make_async_copy(meta_h, gat.at[0, pl.ds(2 * FEAT, 16), left], lsem.at[2]),
    ]
    go(own)
    weights = [pltpu.make_async_copy(h, wt.at[m], lsem.at[3 + m]) for m, h in enumerate((wg_h, wu_h, wd_h))]
    go(weights)
    barrier = pltpu.get_barrier_semaphore()
    for dev in (mate, xpd, xmd, ypd, ymd, zpd, zmd):
        pl.semaphore_signal(barrier, inc=1, device_id=dev, device_id_type=MESH)
    row_i = lax.broadcasted_iota(jnp.int32, (PAIR, PAIR), 0)
    col_i = lax.broadcasted_iota(jnp.int32, (PAIR, PAIR), 1)
    same = (row_i < TOK) == (col_i < TOK)
    tri[...] = jnp.where((row_i < col_i) & same, 1.0, 0.0).astype(BF)
    done(own)
    pl.semaphore_wait(barrier, 7)
    first = [
        rc(gat.at[0, :, left], gat.at[0, :, right], 36, mate),
        rc(gat.at[0, :, left], gat.at[3, :, left], 37, xpd),
        rc(gat.at[0, :, left], gat.at[1, :, left], 38, xmd),
    ]
    go(first)

    def second():
        return [
            rc(gat.at[3, pl.ds(0, FEAT), left], gat.at[2, pl.ds(0, FEAT), left], 39, xpd),
            rc(gat.at[1, pl.ds(FEAT, BLK - FEAT), left], gat.at[2, pl.ds(FEAT, BLK - FEAT), left], 40, xmd),
            rc(gat.at[3, :, left], gat.at[3, :, right], 41, mate),
            rc(gat.at[1, :, left], gat.at[1, :, right], 42, mate),
        ]

    def third():
        return [rc(gat.at[2, :, left], gat.at[2, :, right], 43, mate)]

    def meta_of(r):
        m = gat[r, pl.ds(2 * FEAT, 16), :].astype(F32)
        return m[:8], m[8:]

    def expert_id(e):
        return (node * EXP + e).astype(F32)

    def project(i):
        r, par = (4 - i) % 4, i % 2
        routes, _ = meta_of(r)
        rid = lax.broadcasted_iota(jnp.int32, (16, PAIR), 0)
        lid = lax.broadcasted_iota(jnp.int32, (16, PAIR), 1)
        member = jnp.zeros((16, PAIR), F32)
        for e in range(EXP):
            one = jnp.sum(jnp.where(routes == expert_id(e), 1.0, 0.0), axis=0, keepdims=True)
            member = jnp.where(rid == e, jnp.broadcast_to(one, (16, PAIR)), member)
        before = dot_n(member.astype(BF), tri[...])
        shift = jnp.where(lid < TOK, 0.0, float(CAPS))
        slot[...] = jnp.where(member > 0.5, before + shift, -1.0)
        sid = lax.broadcasted_iota(jnp.int32, (ROWS, PAIR), 0).astype(F32)

        def one_expert(e, carry):
            o = jnp.where(sid == slot[pl.ds(e, 1), :], 1.0, 0.0).astype(BF)
            hot[r, e] = o
            xr = dot_t(o, gat[r, pl.ds(0, FEAT), :]).astype(BF)
            prt[par, 0, e] = dot_n(xr, wt[0, e]).astype(BF)
            prt[par, 1, e] = dot_n(xr, wt[1, e]).astype(BF)
            dr_ = dot_t(o, gat[r, pl.ds(FEAT, FEAT), :]).astype(BF)
            prt[par, 2, e] = dot_n(dr_, wt[2, e]).astype(BF)
            return carry

        lax.fori_loop(0, EXP, one_expert, 0)

    def s1(i):
        p = prt.at[i % 2]
        return [
            rc(p.at[:, y2, lo, ca], r1a.at[0], 0, ymd),
            rc(p.at[:, y2, hi, ca], r1a.at[1], 1, ypd),
            rc(p.at[:, :, lo, lane(z2, HALF)], r1b.at[0], 2, zmd),
            rc(p.at[:, :, hi, lane(z2, HALF)], r1b.at[1], 3, zpd),
        ]

    def s1_add(i):
        p = prt.at[i % 2]
        for m in range(3):
            p[m, ym, lo, ca] = add2(p[m, ym, lo, ca], r1a[0, m])
            p[m, yp, hi, ca] = add2(p[m, yp, hi, ca], r1a[1, m])
            p[m, :, lo, lane(zm, HALF)] = add2(p[m, :, lo, lane(zm, HALF)], r1b[0, m])
            p[m, :, hi, lane(zp, HALF)] = add2(p[m, :, hi, lane(zp, HALF)], r1b[1, m])

    def s2(i):
        p = prt.at[i % 2]
        return [
            rc(p.at[:, yp, :, ca], r2a.at[0], 4, ypd),
            rc(p.at[:, ym, :, ca], r2a.at[1], 5, ymd),
            rc(p.at[:, :, :, lane(zp, HALF)], r2b.at[0], 6, zpd),
            rc(p.at[:, :, :, lane(zm, HALF)], r2b.at[1], 7, zmd),
        ]

    def s2_add(i):
        p = prt.at[i % 2]
        for m in range(3):
            sa[m] = add3(p[m, y, :, ca], r2a[0, m], r2a[1, m]).astype(BF)
            sb[m] = add3(p[m, :, :, lane(z, HALF)], r2b[0, m], r2b[1, m]).astype(BF)

    def s3():
        return [
            rc(sa.at[:, lo, lane(z2, 0)], r3a.at[0], 8, zmd),
            rc(sa.at[:, hi, lane(z2, 0)], r3a.at[1], 9, zpd),
            rc(sb.at[:, y2, lo], r3b.at[0], 10, ymd),
            rc(sb.at[:, y2, hi], r3b.at[1], 11, ypd),
        ]

    def s3_add():
        for m in range(3):
            sa[m, lo, lane(zm, 0)] = add2(sa[m, lo, lane(zm, 0)], r3a[0, m])
            sa[m, hi, lane(zp, 0)] = add2(sa[m, hi, lane(zp, 0)], r3a[1, m])
            sb[m, ym, lo] = add2(sb[m, ym, lo], r3b[0, m])
            sb[m, yp, hi] = add2(sb[m, yp, hi], r3b[1, m])

    def s4():
        return [
            rc(sa.at[:, :, lane(zp, 0)], r4a.at[0], 12, zpd),
            rc(sa.at[:, :, lane(zm, 0)], r4a.at[1], 13, zmd),
            rc(sb.at[:, yp], r4b.at[0], 14, ypd),
            rc(sb.at[:, ym], r4b.at[1], 15, ymd),
        ]

    def activate(i):
        r, par = (4 - i) % 4, i % 2
        routes, gates = meta_of(r)
        match = jnp.where(routes == expert_id(y), 1.0, 0.0)
        gate_row = jnp.sum(match * gates, axis=0, keepdims=True)
        oh = hot[r, y].astype(F32)
        q = jnp.sum(oh * gate_row, axis=1, keepdims=True)
        dots = jnp.zeros((ROWS, 1), F32)
        for k in range(2):
            if k == 0:
                g, u, b = (add3(sa[m, :, lane(z, 0)], r4a[0, m], r4a[1, m]) for m in range(3))
            else:
                g, u, b = (add3(sb[m, y], r4b[0, m], r4b[1, m]) for m in range(3))
            logistic = 1.0 / (1.0 + jnp.exp(-g))
            swished = g * logistic
            hidden = swished * u
            dots = dots + jnp.sum(hidden * b, axis=1, keepdims=True)
            scaled = q * b
            at = lane(z, k * HALF)
            act[par, 0, y, :, at] = (scaled * u * logistic * (1.0 + g * (1.0 - logistic))).astype(BF)
            act[par, 1, y, :, at] = (scaled * swished).astype(BF)
            act[par, 2, y, :, at] = (q * hidden).astype(BF)
        dv[0] = match * jnp.sum(oh * dots, axis=0, keepdims=True)

    def a1(i):
        t = act.at[i % 2]
        az, bz = t.at[:, y, :, lane(z, 0)], t.at[:, y, :, lane(z, HALF)]
        return [rc(az, az, 16, zpd), rc(az, az, 17, zmd), rc(bz, bz, 18, ypd), rc(bz, bz, 19, ymd),
                rc(dv.at[0], dr.at[0], 32, d_z1)]

    def a2(i):
        t = act.at[i % 2]
        v = [t.at[:, y, lo, lane(zm, 0)], t.at[:, y, hi, lane(zp, 0)],
             t.at[:, ym, lo, lane(z, HALF)], t.at[:, yp, hi, lane(z, HALF)]]
        return [rc(v[0], v[0], 20, zpd), rc(v[1], v[1], 21, zmd), rc(v[2], v[2], 22, ypd), rc(v[3], v[3], 23, ymd),
                rc(dv.at[1], dr.at[1], 33, d_z3)]

    def a3(i):
        t = act.at[i % 2]
        ay, bz = t.at[:, y, :, ca], t.at[:, :, :, lane(z, HALF)]
        return [rc(ay, ay, 24, ypd), rc(ay, ay, 25, ymd), rc(bz, bz, 26, zpd), rc(bz, bz, 27, zmd),
                rc(dv.at[2], dr.at[2], 34, d_y1)]

    def a4(i):
        t = act.at[i % 2]
        v = [t.at[:, ym, lo, ca], t.at[:, yp, hi, ca],
             t.at[:, :, lo, lane(zm, HALF)], t.at[:, :, hi, lane(zp, HALF)]]
        return [rc(v[0], v[0], 28, ypd), rc(v[1], v[1], 29, ymd), rc(v[2], v[2], 30, zpd), rc(v[3], v[3], 31, zmd),
                rc(dv.at[3], dr.at[3], 35, d_y3)]

    def dstep(k):
        dv[k + 1] = dv[k] + dr[k]

    def post_a(j):
        r, par = (4 - j) % 4, j % 2
        bk[...] = jnp.zeros_like(bk)

        def one_expert(e, carry):
            rb = dot_t(wt[0, e], act[par, 0, e]) + dot_t(wt[1, e], act[par, 1, e])
            bk[...] += dot_n(rb.astype(BF), hot[r, e])
            return carry

        lax.fori_loop(0, EXP, one_expert, 0)
        cb[r, pl.ds(0, FEAT), :] = bk[...].astype(BF)
        cb[r, pl.ds(FEAT, 16), :] = jnp.concatenate([df[par], jnp.zeros((8, PAIR), F32)], 0).astype(BF)

    def post_b(j):
        r, par = (4 - j) % 4, j % 2

        def one_expert(e, carry):
            xt = dot_t(gat[r, pl.ds(0, FEAT), :], hot[r, e]).astype(BF)
            acc[0, e] = (acc[0, e].astype(F32) + dot_n(xt, act[par, 0, e])).astype(BF)
            acc[1, e] = (acc[1, e].astype(F32) + dot_n(xt, act[par, 1, e])).astype(BF)
            dt = dot_t(gat[r, pl.ds(FEAT, FEAT), :], hot[r, e]).astype(BF)
            acc[2, e] = (acc[2, e].astype(F32) + dot_n(dt, act[par, 2, e])).astype(BF)
            return carry

        lax.fori_loop(0, EXP, one_expert, 0)

    def c1(r):
        return [pltpu.make_async_remote_copy(
            src_ref=cb.at[r, :, right], dst_ref=c1r.at[r], send_sem=dsem.at[r], recv_sem=esem.at[r],
            device_id=mate, device_id_type=MESH)]

    def c2():
        return [rc(cs.at[2, pl.ds(0, CUT)], c2a, 44, xpd), rc(cs.at[2, pl.ds(CUT, CROWS - CUT)], c2b, 45, xmd)]

    def c3(k):
        return rc(cs.at[1], c3r.at[0], 46, xpd) if k == 0 else rc(cs.at[3], c3r.at[1], 47, xmd)

    done(first[:1])
    done(weights)
    project(jnp.int32(0))
    go(s1(0))

    def body(i, carry):
        rs = i <= 3
        ag = i >= 1

        @pl.when(ag)
        def _():
            go(a1(i - 1))

        @pl.when(i == 1)
        def _():
            done(third())

        @pl.when((i >= 1) & (i <= 2))
        def _():
            project(i + 1)

        @pl.when(ag)
        def _():
            done(a1(i - 1))
            dstep(0)
            go(a2(i - 1))

        @pl.when(rs)
        def _():
            done(s1(i))
            s1_add(i)
            go(s2(i))

        @pl.when(i == 0)
        def _():
            done(first[1:])
            go(second())

            def clear(e, cc):
                for m in range(3):
                    acc[m, e] = jnp.zeros((FEAT, HID), BF)
                return cc

            lax.fori_loop(0, EXP, clear, 0)
            copies = second()
            done(copies[2:])
            project(jnp.int32(1))
            done(copies[:2])
            go(third())

        @pl.when(ag)
        def _():
            done(a2(i - 1))
            dstep(1)
            go(a3(i - 1))

        @pl.when(i >= 2)
        def _():
            post_a(i - 2)
            go(c1((6 - i) % 4))
            post_b(i - 2)

        @pl.when(rs)
        def _():
            done(s2(i))
            s2_add(i)
            go(s3())

        @pl.when(ag)
        def _():
            done(a3(i - 1))
            dstep(2)
            go(a4(i - 1))

        @pl.when(rs)
        def _():
            done(s3())
            s3_add()
            go(s4())

        @pl.when(i <= 2)
        def _():
            go(s1(i + 1))

        @pl.when(rs)
        def _():
            done(s4())
            activate_guard(i)

        @pl.when(i >= 2)
        def _():
            r = (6 - i) % 4
            done(c1(r))
            cs[r] = add2(cb[r, :, left], c1r[r])

        @pl.when(i == 4)
        def _():
            go(c2())

        return carry

    def activate_guard(i):
        @pl.when(i >= 1)
        def _():
            done(a4(i - 1))
            dstep(3)
            df[(i - 1) % 2] = dv[4]

        activate(i)

    lax.fori_loop(0, 5, body, 0)
    done(a4(3))
    dstep(3)
    df[1] = dv[4]
    post_a(3)
    go(c1(1))
    done(c2())
    cs[3, pl.ds(CUT, CROWS - CUT), :] = add2(cs[3, pl.ds(CUT, CROWS - CUT), :], c2b[...])
    c3(1).start()
    done(c1(1))
    cs[1] = add2(cb[1, :, left], c1r[1])
    cs[1, pl.ds(0, CUT), :] = add2(cs[1, pl.ds(0, CUT), :], c2a[...])
    c3(0).start()
    post_b(3)
    outs = [pltpu.make_async_copy(acc.at[m], h, lsem.at[3 + m]) for m, h in enumerate((og_h, ou_h, od_h))]
    go(outs)

    ld[...] = jnp.zeros_like(ld)
    eid = lax.broadcasted_iota(jnp.int32, (ALL_EXPERTS, 128), 0)

    def one_block(b, carry):
        r = (b // 2 - x + 4) % 4
        cc = (b % 2 + c) % 2
        m = gat[r, pl.ds(2 * FEAT, 16), pl.ds(pl.multiple_of(cc * TOK, TOK), TOK)].astype(F32)
        routes, gates = m[:8], m[8:]
        tot = jnp.zeros((ALL_EXPERTS, 128), F32)
        for e in range(ALL_EXPERTS):
            s = jnp.sum(jnp.where(routes == float(e), gates, 0.0), axis=0, keepdims=True)
            s = jnp.sum(s, axis=1, keepdims=True)
            tot = jnp.where(eid == e, jnp.broadcast_to(s, (ALL_EXPERTS, 128)), tot)
        ld[...] += tot
        return carry

    lax.fori_loop(0, 8, one_block, 0)
    ld[...] = ld[...] * (1.0 / 64.0)
    done([c3(0), c3(1)])
    total = add3(cs[0], c3r[0], c3r[1]).astype(BF)
    gt[...] = total[:FEAT]
    gg[...] = total[FEAT:]
    last = [
        pltpu.make_async_copy(gt, gt_h, lsem.at[0]),
        pltpu.make_async_copy(gg, gg_h, lsem.at[1]),
        pltpu.make_async_copy(ld, load_h, lsem.at[2]),
    ]
    go(last)
    done(last)
    done(outs)


def on_device(tokens, grad_out, gates, routes, w_gate, w_up, w_down):
    meta = jnp.concatenate([routes.T.astype(BF), gates.T], 0)
    shape = jax.ShapeDtypeStruct
    any_ = pl.BlockSpec(memory_space=pl.ANY)
    V = pltpu.VMEM
    w_shape = (EXP, FEAT, HID)
    scratch = [
        V((3, *w_shape), BF), V((4, BLK, PAIR), BF), V((PAIR, PAIR), BF), V((4, EXP, ROWS, PAIR), BF),
        V((16, PAIR), F32), V((2, 3, EXP, ROWS, HID), BF),
        V((2, 3, CAPS, HALF), BF), V((2, 3, EXP, CAPS, 128), BF),
        V((2, 3, ROWS, HALF), BF), V((2, 3, EXP, ROWS, 128), BF),
        V((3, ROWS, HALF), BF), V((3, EXP, ROWS, 128), BF),
        V((2, 3, CAPS, 128), BF), V((2, 3, CAPS, 128), BF),
        V((2, 3, ROWS, 128), BF), V((2, 3, ROWS, 128), BF),
        V((2, 3, EXP, ROWS, HID), BF), V((5, 8, PAIR), F32), V((4, 8, PAIR), F32), V((2, 8, PAIR), F32),
        V((3, *w_shape), BF), V((FEAT, PAIR), F32), V((4, CROWS, PAIR), BF), V((4, CROWS, TOK), BF),
        V((4, CROWS, TOK), BF), V((CUT, TOK), BF), V((CROWS - CUT, TOK), BF), V((2, CROWS, TOK), BF),
        V((FEAT, TOK), BF), V((16, TOK), BF), V((ALL_EXPERTS, 128), F32),
        pltpu.SemaphoreType.DMA((6,)), pltpu.SemaphoreType.DMA((48,)), pltpu.SemaphoreType.DMA((48,)),
        pltpu.SemaphoreType.DMA((4,)), pltpu.SemaphoreType.DMA((4,)),
    ]
    gt, gg, ld, og, ou, od = pl.pallas_call(
        kernel,
        name="expert_backward",
        out_shape=(
            shape((FEAT, TOK), BF), shape((16, TOK), BF), shape((ALL_EXPERTS, 128), F32),
            shape(w_shape, BF), shape(w_shape, BF), shape(w_shape, BF),
        ),
        in_specs=[any_] * 6,
        out_specs=[any_] * 6,
        scratch_shapes=scratch,
        compiler_params=pltpu.CompilerParams(
            collective_id=0, has_side_effects=True, vmem_limit_bytes=66_900_000
        ),
    )(meta, tokens.T, grad_out.T, w_gate, w_up, jnp.transpose(w_down, (0, 2, 1)))
    return gt.T, gg[:8].T, og, ou, jnp.transpose(od, (0, 2, 1)), ld[:, 0]


def solution(mesh):
    in_specs = (
        P("node", "local"),
        P("node", "local"),
        P("node", None),
        P("node", None),
        P("node", "local", None),
        P("node", "local", None),
        P("node", None, "local"),
    )
    out_specs = (
        P("node", "local"),
        P("node", None),
        P("node", "local", None),
        P("node", "local", None),
        P("node", None, "local"),
        P(),
    )
    return jax.shard_map(
        on_device, mesh=mesh, in_specs=in_specs, out_specs=out_specs, check_vma=False
    )
```

time: 425 us -> 227 us (0.53)
  waiting for transfers between devices: 228 us -> 0 us
  Pallas kernels: 0 us -> 211 us
  local copies, waits for them, and re-layouts: 70.4 us -> 13.9 us
  matrix products: 55 us -> 0 us
  starting transfers between devices: 30.1 us -> 0 us
  other arithmetic: 25.9 us -> 1.99 us
  between operations: 14.2 us -> 0.65 us
    pallas_call x0 -> x1, Pallas kernels: none -> 211 us  [on_device(): pl.pallas_call(kernel, name='expert_backward', out_shape=(shape((FEAT, TO...]
    psum x1 -> x0, waiting for transfers between devices: 180 us -> none  [on_device(): lax.psum(up_pre.astype(jnp.bfloat16), 'local').astype(jnp.float32)]
    dot_general x8 -> x0, matrix products: 55 us -> none  [the longest x1 10.1 us: on_device(): jnp.einsum('sjch,sjcd->jhd', weighted, grad_rows, preferred_element_type=...]
    all_to_all x6 -> x0, waiting for transfers between devices: 48.2 us -> none  [the longest x1 23.4 us: on_device(): lax.all_to_all(send_tokens, 'node', split_axis=0, concat_axis=0, tiled=True)]
    gather x4 -> x0, local copies, waits for them, and re-layouts: 38.6 us -> none  [the longest x1 13.1 us: on_device(): returned_products.reshape(experts * capacity)[target]]
    all_to_all x6 -> x0, starting transfers between devices: 30.1 us -> none  [the longest x1 5.92 us: on_device(): lax.all_to_all(send_tokens, 'node', split_axis=0, concat_axis=0, tiled=True)]
    scatter x2 -> x0, local copies, waits for them, and re-layouts: 22.6 us -> none  [the longest x1 14.6 us: on_device(): jnp.zeros((experts * capacity,), jnp.bfloat16).at[target].set(flat_gates)]
    reduce_sum x5 -> x0, other arithmetic: 15.2 us -> none  [the longest x1 12 us: activation_grads(): products = jnp.sum(hidden * back_hidden, axis=-1)]
  transfers between devices with their start and end apart: 7 -> 0, of which waited for: 4 -> 0; matrix products, arithmetic and copies ran while one was open for 20% -> 0% of each run, Pallas kernels for 0% -> 0%
where the time goes in v1:
time: 227 us
  Pallas kernels  211 us (93%)
  local copies, waits for them, and re-layouts  13.9 us (6%)
    pallas_call x1, Pallas kernels, on_device(): pl.pallas_call(kernel, name='expert_backward', out_shape=(shape((FEAT, TO...  211 us
    unnamed x8, local copies, waits for them, and re-layouts  11.3 us

profile of v1, /device:TPU:1, one launch (start us, length us, event | category | flops | bytes accessed | tf_op | source)
XLA Modules:
  0.0 227.1 jit_solution(14298559531833865941)
XLA Ops:
  0.6 0.7 convert_bitcast_fusion
  1.3 1.3 pad_maximum_fusion.meta_h
  2.6 210.7 %expert_backward.1 = (bf16[448,256]{1,0:T(8,128)(2,1)}, bf16[16,256]{1,0:T(8,128)(2,1)}, f32[32,128]{1,0:T(8,128)}, bf16[4,448,1024]{2,1,0:T(8,128)(2,1)}, bf16[...) custom-call(bf16[16,256]{1,0:T(8,128)(2,1)} %pad_maximum_fusion.meta_h, bf16[448,256]{1,0:T(8,128)(2,1)} %bitcast.13, ...), custom_call_target="tpu_custom_call" | custom-call | tf_op jit(solution)/shard_map/expert_backward/pallas_call | solution.py:476
  213.3 1.3 slice_reduce_fusion
  214.6 1.3 slice_bitcast_fusion
  215.9 1.6 copy.17
  217.5 0.0 copy-start.1
  217.5 4.4 %copy.18 = bf16[4,448,1024]{2,1,0:T(8,128)(2,1)} copy(bf16[4,448,1024]{2,1,0:T(8,128)(2,1)} %get-tuple-element.26) | data formatting | bytes 7340032
  221.9 0.0 copy-done.1
  221.9 0.0 copy-start
  222.0 1.9 copy.19
  223.8 1.5 copy-done
  225.3 1.8 copy.20
Async XLA Ops:
  217.5 4.4 %copy-start.1 = (bf16[4,448,1024]{2,1,0:T(8,128)(2,1)S(1)}, bf16[4,448,1024]{2,1,0:T(8,128)(2,1)}, u32[]{:S(2)}) copy-start(bf16[4,448,1024]{2,1,0:T(8,128)(2,1)} %get-tuple-element.27) | copy-start | bytes 11010052
  221.9 3.4 %copy-start = (bf16[4,448,1024]{2,1,0:T(8,128)(2,1)S(1)}, bf16[4,448,1024]{2,1,0:T(8,128)(2,1)}, u32[]{:S(2)}) copy-start(bf16[4,448,1024]{2,1,0:T(8,128)(2,1)} %get-tuple-element.16) | copy-start | bytes 11010052

commit v2 on v0

v2 whole, which is shorter than its diff:
```python
import jax
import jax.numpy as jnp
from jax import lax
from jax.experimental import pallas as pl
from jax.experimental.pallas import tpu as pltpu
from jax.sharding import PartitionSpec as P

BF = jnp.bfloat16
F32 = jnp.float32
MESH = pl.DeviceIdType.MESH
FEAT, TOK, HID, CAPS, EXP = 448, 256, 1024, 80, 4
PAIR = 2 * TOK
ROWS = 2 * CAPS
NLO = 48
HALF = HID // 2
BLK = 2 * FEAT + 16
CROWS = FEAT + 16
CUT = 240
ALL_EXPERTS = 32


def dot_t(a, b):
    return lax.dot_general(a, b, (((1,), (1,)), ((), ())), preferred_element_type=F32)


def dot_n(a, b):
    return jnp.dot(a, b, preferred_element_type=F32)


def add2(a, b):
    return (a.astype(F32) + b.astype(F32)).astype(BF)


def add3(a, b, c):
    return a.astype(F32) + b.astype(F32) + c.astype(F32)


class Part:
    def __init__(self, r, rows, lanes, local_rows, cut, bufs, base, par, dpar):
        self.r, self.rows, self.lanes, self.n, self.cut = r, rows, lanes, local_rows, cut
        self.width = lanes[1] - lanes[0]
        (self.p, self.r1a, self.r1b, self.r2a, self.r2b, self.sa, self.sb,
         self.r3a, self.r3b, self.r4a, self.r4b, self.t) = bufs
        self.base, self.par, self.d = base, par, dpar
        self.lo, self.hi = pl.ds(0, cut), pl.ds(cut, local_rows - cut)
        self.nlo, self.nhi = pl.ds(0, cut), pl.ds(0, local_rows - cut)
        self.all = pl.ds(0, local_rows)
        self.ln = pl.ds(lanes[0], self.width)
        self.rw = pl.ds(rows[0], local_rows)


def kernel(
    routes_h, gates_h, tok_h, dy_h, wg_h, wu_h, wd_h,
    gt, gg, ld, acc0, acc1, acc2,
    wt, gat, tri, hot, slot, rbuf, gbuf, prt, r1a, r1b, r2a, r2b, sa, sb, r3a, r3b, r4a, r4b, act,
    prt_h, r1a_h, r1b_h, r2a_h, r2b_h, sa_h, sb_h, r3a_h, r3b_h, r4a_h, r4b_h, act_h,
    dv, dr, df, bk, cb, c1r, cs, c2a, c2b, c3r,
    lsem, ssem, rsem,
):
    acc = (acc0, acc1, acc2)
    node, local = lax.axis_index("node"), lax.axis_index("local")
    x, c = node // 2, node % 2
    y, z = local // 4, local % 4
    yp, ym, y2 = (y + 1) % 4, (y + 3) % 4, (y + 2) % 4
    zp, zm, z2 = (z + 1) % 4, (z + 3) % 4, (z + 2) % 4

    def at_x(k):
        return (((x + k) % 4) * 2 + c, local)

    def at_yz(a, b):
        return (node, a * 4 + b)

    mate = (x * 2 + 1 - c, local)
    xpd, xmd = at_x(1), at_x(3)
    ypd, ymd, zpd, zmd = at_yz(yp, z), at_yz(ym, z), at_yz(y, zp), at_yz(y, zm)
    d_z1, d_z3 = at_yz(y, z + 1 - 2 * (z % 2)), at_yz(y, 3 - z)
    d_y1, d_y3 = at_yz(y + 1 - 2 * (y % 2), z), at_yz(3 - y, z)

    def rc(src, dst, k, dev):
        return pltpu.make_async_remote_copy(
            src_ref=src, dst_ref=dst, send_sem=ssem.at[k], recv_sem=rsem.at[k],
            device_id=dev, device_id_type=MESH,
        )

    def go(copies):
        for cp in copies:
            cp.start()

    def done(copies):
        for cp in copies:
            cp.wait()

    def lane(q, base):
        return pl.ds(pl.multiple_of(base + 128 * q, 128), 128)

    left, right = pl.ds(0, TOK), pl.ds(TOK, TOK)
    ca = pl.ds(0, HALF)
    tok_rows, dy_rows, meta_rows = pl.ds(0, FEAT), pl.ds(FEAT, FEAT), pl.ds(2 * FEAT, 16)

    own = [
        pltpu.make_async_copy(routes_h, rbuf, lsem.at[0]),
        pltpu.make_async_copy(gates_h, gbuf, lsem.at[1]),
        pltpu.make_async_copy(tok_h, gat.at[0, tok_rows, left], lsem.at[2]),
        pltpu.make_async_copy(dy_h, gat.at[0, dy_rows, left], lsem.at[3]),
    ]
    go(own)
    weights = [pltpu.make_async_copy(h, wt.at[m], lsem.at[4 + m]) for m, h in enumerate((wg_h, wu_h, wd_h))]
    go(weights)
    barrier = pltpu.get_barrier_semaphore()
    for dev in (mate, xpd, xmd, ypd, ymd, zpd, zmd):
        pl.semaphore_signal(barrier, inc=1, device_id=dev, device_id_type=MESH)
    done(own[:2])
    gat[0, meta_rows, left] = jnp.concatenate([rbuf[...].astype(F32), gbuf[...].astype(F32)], 0).astype(BF)
    row_i = lax.broadcasted_iota(jnp.int32, (TOK, TOK), 0)
    col_i = lax.broadcasted_iota(jnp.int32, (TOK, TOK), 1)
    tri[...] = jnp.where(row_i < col_i, 1.0, 0.0).astype(BF)
    done(own[2:])
    pl.semaphore_wait(barrier, 7)
    first = [
        rc(gat.at[0, :, left], gat.at[0, :, right], 0, mate),
        rc(gat.at[0, :, left], gat.at[3, :, left], 1, xpd),
        rc(gat.at[0, :, left], gat.at[1, :, left], 2, xmd),
    ]
    second = [
        rc(gat.at[3, tok_rows, left], gat.at[2, tok_rows, left], 3, xpd),
        rc(gat.at[1, pl.ds(FEAT, BLK - FEAT), left], gat.at[2, pl.ds(FEAT, BLK - FEAT), left], 4, xmd),
        rc(gat.at[3, :, left], gat.at[3, :, right], 5, mate),
        rc(gat.at[1, :, left], gat.at[1, :, right], 6, mate),
    ]
    third = [rc(gat.at[2, :, left], gat.at[2, :, right], 7, mate)]
    go(first)

    def bufs(par):
        return (prt.at[par], r1a, r1b, r2a, r2b, sa, sb, r3a, r3b, r4a, r4b, act.at[par])

    half_bufs = (prt_h, r1a_h, r1b_h, r2a_h, r2b_h, sa_h, sb_h, r3a_h, r3b_h, r4a_h, r4b_h, act_h)
    k0 = Part(0, (0, CAPS), (0, TOK), CAPS, NLO, bufs(0), 20, 0, 0)
    k1 = Part(3, (0, ROWS), (0, PAIR), ROWS, CAPS, bufs(1), 20, 1, 1)
    k2 = Part(2, (0, ROWS), (0, PAIR), ROWS, CAPS, bufs(0), 20, 0, 0)
    k3 = Part(1, (0, ROWS), (0, PAIR), ROWS, CAPS, bufs(1), 20, 1, 1)
    kh = Part(0, (CAPS, ROWS), (TOK, PAIR), CAPS, NLO, half_bufs, 64, 0, 2)

    def meta_of(k):
        m = gat[k.r, meta_rows, k.ln].astype(F32)
        return m[:8], m[8:]

    def expert_id(e):
        return (node * EXP + e).astype(F32)

    def project(k):
        routes, _ = meta_of(k)
        wide = (16, k.width)
        rid = lax.broadcasted_iota(jnp.int32, wide, 0)
        member = jnp.zeros(wide, F32)
        for e in range(EXP):
            one = jnp.sum(jnp.where(routes == expert_id(e), 1.0, 0.0), axis=0, keepdims=True)
            member = jnp.where(rid == e, jnp.broadcast_to(one, wide), member)
        for h in range(k.width // TOK):
            mine = member[:, h * TOK : (h + 1) * TOK]
            before = dot_n(mine.astype(BF), tri[...])
            slot[:, pl.ds(h * TOK, TOK)] = jnp.where(mine > 0.5, before + float(CAPS * h), -1.0)
        sid = lax.broadcasted_iota(jnp.int32, (k.n, k.width), 0).astype(F32)

        def one_expert(e, carry):
            o = jnp.where(sid == slot[pl.ds(e, 1), pl.ds(0, k.width)], 1.0, 0.0).astype(BF)
            hot[k.r, e, k.rw, k.ln] = o
            xr = dot_t(o, gat[k.r, tok_rows, k.ln]).astype(BF)
            k.p[0, e, k.all] = dot_n(xr, wt[0, e]).astype(BF)
            k.p[1, e, k.all] = dot_n(xr, wt[1, e]).astype(BF)
            gr = dot_t(o, gat[k.r, dy_rows, k.ln]).astype(BF)
            k.p[2, e, k.all] = dot_n(gr, wt[2, e]).astype(BF)
            return carry

        lax.fori_loop(0, EXP, one_expert, 0)

    def s1(k):
        p, b = k.p, k.base
        return [
            rc(p.at[:, y2, k.lo, ca], k.r1a.at[0, :, k.nlo], b, ymd),
            rc(p.at[:, y2, k.hi, ca], k.r1a.at[1, :, k.nhi], b + 1, ypd),
            rc(p.at[:, :, k.lo, lane(z2, HALF)], k.r1b.at[0, :, :, k.nlo], b + 2, zmd),
            rc(p.at[:, :, k.hi, lane(z2, HALF)], k.r1b.at[1, :, :, k.nhi], b + 3, zpd),
        ]

    def s1_add(k):
        p = k.p
        for m in range(3):
            p[m, ym, k.lo, ca] = add2(p[m, ym, k.lo, ca], k.r1a[0, m, k.nlo])
            p[m, yp, k.hi, ca] = add2(p[m, yp, k.hi, ca], k.r1a[1, m, k.nhi])
            p[m, :, k.lo, lane(zm, HALF)] = add2(p[m, :, k.lo, lane(zm, HALF)], k.r1b[0, m, :, k.nlo])
            p[m, :, k.hi, lane(zp, HALF)] = add2(p[m, :, k.hi, lane(zp, HALF)], k.r1b[1, m, :, k.nhi])

    def s2(k):
        p, b = k.p, k.base + 4
        return [
            rc(p.at[:, yp, k.all, ca], k.r2a.at[0, :, k.all], b, ypd),
            rc(p.at[:, ym, k.all, ca], k.r2a.at[1, :, k.all], b + 1, ymd),
            rc(p.at[:, :, k.all, lane(zp, HALF)], k.r2b.at[0, :, :, k.all], b + 2, zpd),
            rc(p.at[:, :, k.all, lane(zm, HALF)], k.r2b.at[1, :, :, k.all], b + 3, zmd),
        ]

    def s2_add(k):
        p = k.p
        for m in range(3):
            k.sa[m, k.all] = add3(p[m, y, k.all, ca], k.r2a[0, m, k.all], k.r2a[1, m, k.all]).astype(BF)
            k.sb[m, :, k.all] = add3(
                p[m, :, k.all, lane(z, HALF)], k.r2b[0, m, :, k.all], k.r2b[1, m, :, k.all]
            ).astype(BF)

    def s3(k):
        b = k.base + 8
        return [
            rc(k.sa.at[:, k.lo, lane(z2, 0)], k.r3a.at[0, :, k.nlo], b, zmd),
            rc(k.sa.at[:, k.hi, lane(z2, 0)], k.r3a.at[1, :, k.nhi], b + 1, zpd),
            rc(k.sb.at[:, y2, k.lo], k.r3b.at[0, :, k.nlo], b + 2, ymd),
            rc(k.sb.at[:, y2, k.hi], k.r3b.at[1, :, k.nhi], b + 3, ypd),
        ]

    def s3_add(k):
        a, b = k.sa, k.sb
        for m in range(3):
            a[m, k.lo, lane(zm, 0)] = add2(a[m, k.lo, lane(zm, 0)], k.r3a[0, m, k.nlo])
            a[m, k.hi, lane(zp, 0)] = add2(a[m, k.hi, lane(zp, 0)], k.r3a[1, m, k.nhi])
            b[m, ym, k.lo] = add2(b[m, ym, k.lo], k.r3b[0, m, k.nlo])
            b[m, yp, k.hi] = add2(b[m, yp, k.hi], k.r3b[1, m, k.nhi])

    def s4(k):
        b = k.base + 12
        return [
            rc(k.sa.at[:, k.all, lane(zp, 0)], k.r4a.at[0, :, k.all], b, zpd),
            rc(k.sa.at[:, k.all, lane(zm, 0)], k.r4a.at[1, :, k.all], b + 1, zmd),
            rc(k.sb.at[:, yp, k.all], k.r4b.at[0, :, k.all], b + 2, ypd),
            rc(k.sb.at[:, ym, k.all], k.r4b.at[1, :, k.all], b + 3, ymd),
        ]

    def activate(k):
        routes, gates = meta_of(k)
        match = jnp.where(routes == expert_id(y), 1.0, 0.0)
        gate_row = jnp.sum(match * gates, axis=0, keepdims=True)
        oh = hot[k.r, y, k.rw, k.ln].astype(F32)
        q = jnp.sum(oh * gate_row, axis=1, keepdims=True)
        dots = jnp.zeros((k.n, 1), F32)
        for h in range(2):
            if h == 0:
                g, u, b = (
                    add3(k.sa[m, k.all, lane(z, 0)], k.r4a[0, m, k.all], k.r4a[1, m, k.all]) for m in range(3)
                )
            else:
                g, u, b = (add3(k.sb[m, y, k.all], k.r4b[0, m, k.all], k.r4b[1, m, k.all]) for m in range(3))
            logistic = 1.0 / (1.0 + jnp.exp(-g))
            swished = g * logistic
            hidden = swished * u
            dots = dots + jnp.sum(hidden * b, axis=1, keepdims=True)
            scaled = q * b
            at = lane(z, h * HALF)
            k.t[0, y, k.all, at] = (scaled * u * logistic * (1.0 + g * (1.0 - logistic))).astype(BF)
            k.t[1, y, k.all, at] = (scaled * swished).astype(BF)
            k.t[2, y, k.all, at] = (q * hidden).astype(BF)
        dv[k.d, 0, :, pl.ds(0, k.width)] = match * jnp.sum(oh * dots, axis=0, keepdims=True)

    def share(k, step, b, dev):
        at = pl.ds(0, k.width)
        return rc(dv.at[k.d, step, :, at], dr.at[k.d, step, :, at], b, dev)

    def a1(k):
        t, b = k.t, k.base + 16
        az, bz = t.at[:, y, k.all, lane(z, 0)], t.at[:, y, k.all, lane(z, HALF)]
        return [rc(az, az, b, zpd), rc(az, az, b + 1, zmd), rc(bz, bz, b + 2, ypd), rc(bz, bz, b + 3, ymd),
                share(k, 0, b + 4, d_z1)]

    def a2(k):
        t, b = k.t, k.base + 21
        v = [t.at[:, y, k.lo, lane(zm, 0)], t.at[:, y, k.hi, lane(zp, 0)],
             t.at[:, ym, k.lo, lane(z, HALF)], t.at[:, yp, k.hi, lane(z, HALF)]]
        return [rc(v[0], v[0], b, zpd), rc(v[1], v[1], b + 1, zmd), rc(v[2], v[2], b + 2, ypd),
                rc(v[3], v[3], b + 3, ymd), share(k, 1, b + 4, d_z3)]

    def a3(k):
        t, b = k.t, k.base + 26
        ay, bz = t.at[:, y, k.all, ca], t.at[:, :, k.all, lane(z, HALF)]
        return [rc(ay, ay, b, ypd), rc(ay, ay, b + 1, ymd), rc(bz, bz, b + 2, zpd), rc(bz, bz, b + 3, zmd),
                share(k, 2, b + 4, d_y1)]

    def a4(k):
        t, b = k.t, k.base + 31 + 5 * k.par
        v = [t.at[:, ym, k.lo, ca], t.at[:, yp, k.hi, ca],
             t.at[:, :, k.lo, lane(zm, HALF)], t.at[:, :, k.hi, lane(zp, HALF)]]
        return [rc(v[0], v[0], b, ypd), rc(v[1], v[1], b + 1, ymd), rc(v[2], v[2], b + 2, zpd),
                rc(v[3], v[3], b + 3, zmd), share(k, 3, b + 4, d_y3)]

    def dstep(k, step):
        at = pl.ds(0, k.width)
        dv[k.d, step + 1, :, at] = dv[k.d, step, :, at] + dr[k.d, step, :, at]

    def do_s1(k):
        done(s1(k))
        s1_add(k)
        go(s2(k))

    def do_s2(k):
        done(s2(k))
        s2_add(k)
        go(s3(k))

    def do_s3(k):
        done(s3(k))
        s3_add(k)
        go(s4(k))

    def do_a1(k):
        done(a1(k))
        dstep(k, 0)
        go(a2(k))

    def do_a2(k):
        done(a2(k))
        dstep(k, 1)
        go(a3(k))

    def do_a3(k):
        done(a3(k))
        dstep(k, 2)

    def post_a(k):
        done(a4(k))
        dstep(k, 3)
        at = pl.ds(0, k.width)
        bk[:, at] = jnp.zeros((FEAT, k.width), F32)

        def one_expert(e, carry):
            rb = dot_t(wt[0, e], k.t[0, e, k.all]) + dot_t(wt[1, e], k.t[1, e, k.all])
            bk[:, at] += dot_n(rb.astype(BF), hot[k.r, e, k.rw, k.ln])
            return carry

        lax.fori_loop(0, EXP, one_expert, 0)
        cb[k.r, tok_rows, k.ln] = bk[:, at].astype(BF)
        cb[k.r, pl.ds(FEAT, 16), k.ln] = jnp.concatenate(
            [dv[k.d, 4, :, at], jnp.zeros((8, k.width), F32)], 0
        ).astype(BF)

    def post_b(k, fresh=False):
        def one_expert(e, carry):
            xt = dot_t(gat[k.r, tok_rows, k.ln], hot[k.r, e, k.rw, k.ln]).astype(BF)
            gr = dot_t(gat[k.r, dy_rows, k.ln], hot[k.r, e, k.rw, k.ln]).astype(BF)
            for m, side in enumerate((xt, xt, gr)):
                new = dot_n(side, k.t[m, e, k.all])
                acc[m][e] = (new if fresh else acc[m][e].astype(F32) + new).astype(BF)
            return carry

        lax.fori_loop(0, EXP, one_expert, 0)

    def c1(r):
        return [rc(cb.at[r, :, right], c1r.at[r], 8 + r, mate)]

    def do_c1(r):
        done(c1(r))
        cs[r] = add2(cb[r, :, left], c1r[r])

    c2 = [rc(cs.at[2, pl.ds(0, CUT)], c2a, 12, xpd), rc(cs.at[2, pl.ds(CUT, CROWS - CUT)], c2b, 13, xmd)]
    c3 = [rc(cs.at[1], c3r.at[0], 14, xpd), rc(cs.at[3], c3r.at[1], 15, xmd)]

    done(weights)
    project(k0)
    go(s1(k0))
    done(first[:1])
    project(kh)
    go(s1(kh))
    do_s1(k0)
    do_s1(kh)
    done(first[1:])
    go(second)
    done(second[2:3])
    project(k1)
    do_s2(k0)
    go(s1(k1))
    do_s2(kh)
    do_s3(k0)
    do_s3(kh)
    done(s4(k0))
    activate(k0)
    go(a1(k0))
    do_s1(k1)
    done(s4(kh))
    activate(kh)
    do_a1(k0)
    done(second[:2])
    done(second[3:])
    go(third)
    do_a2(k0)

    done(third)
    project(k2)
    do_s2(k1)
    do_a3(k0)
    do_s3(k1)
    go(s1(k2))
    go(a4(k0))
    done(s4(k1))
    activate(k1)
    go(a1(k1))

    done(s1(k2))
    s1_add(k2)
    do_a1(k1)
    go(s2(k2))
    do_a2(k1)
    post_a(k0)
    post_b(k0, True)
    project(k3)
    do_s2(k2)
    do_a3(k1)
    do_s3(k2)
    go(s1(k3))
    go(a4(k1))
    done(s4(k2))
    activate(k2)
    go(a1(k2))

    done(s1(k3))
    s1_add(k3)
    do_a1(k2)
    go(s2(k3))
    do_a2(k2)
    post_a(k1)
    go(c1(3))
    post_b(k1)
    do_s2(k3)
    do_a3(k2)
    do_s3(k3)
    go(a4(k2))
    done(s4(k3))
    activate(k3)
    go(a1(k3))

    do_c1(3)
    do_a1(k3)
    do_a2(k3)
    go(a1(kh))
    post_a(k2)
    go(c1(2))
    post_b(k2)
    do_c1(2)
    go(c2)
    do_a3(k3)
    go(a4(k3))
    do_a1(kh)
    done(c2)
    cs[3, pl.ds(CUT, CROWS - CUT), :] = add2(cs[3, pl.ds(CUT, CROWS - CUT), :], c2b[...])
    c3[1].start()
    do_a2(kh)
    post_a(k3)
    go(c1(1))
    do_c1(1)
    cs[1, pl.ds(0, CUT), :] = add2(cs[1, pl.ds(0, CUT), :], c2a[...])
    c3[0].start()
    do_a3(kh)
    go(a4(kh))
    post_b(k3)
    post_a(kh)
    go(c1(0))
    post_b(kh)

    eid = lax.broadcasted_iota(jnp.int32, (1, ALL_EXPERTS), 1)
    ld[...] = jnp.zeros_like(ld)

    def one_block(b, carry):
        r = (b // 2 - x + 4) % 4
        cc = (b % 2 + c) % 2
        m = gat[r, meta_rows, pl.ds(pl.multiple_of(cc * TOK, TOK), TOK)].astype(F32)
        routes, gates = m[:8], m[8:]
        tot = jnp.zeros((1, ALL_EXPERTS), F32)
        for e in range(ALL_EXPERTS):
            s = jnp.sum(jnp.where(routes == float(e), gates, 0.0), axis=0, keepdims=True)
            s = jnp.sum(s, axis=1, keepdims=True)
            tot = jnp.where(eid == e, jnp.broadcast_to(s, (1, ALL_EXPERTS)), tot)
        ld[...] += tot
        return carry

    lax.fori_loop(0, 8, one_block, 0)
    ld[...] = ld[...] * (1.0 / 64.0)
    do_c1(0)
    done(c3)
    total = add3(cs[0], c3r[0], c3r[1])
    gt[...] = total[:FEAT].astype(BF)
    gg[...] = total[FEAT : FEAT + 8].astype(BF)


def on_device(tokens, grad_out, gates, routes, w_gate, w_up, w_down):
    any_ = pl.BlockSpec(memory_space=pl.ANY)
    V = pltpu.VMEM
    w_shape = (EXP, FEAT, HID)

    def comm(copies, rows, cut):
        lead = () if copies is None else (copies,)
        return [
            V((*lead, 3, EXP, rows, HID), BF),
            V((2, 3, cut, HALF), BF), V((2, 3, EXP, cut, 128), BF),
            V((2, 3, rows, HALF), BF), V((2, 3, EXP, rows, 128), BF),
            V((3, rows, HALF), BF), V((3, EXP, rows, 128), BF),
            V((2, 3, cut, 128), BF), V((2, 3, cut, 128), BF),
            V((2, 3, rows, 128), BF), V((2, 3, rows, 128), BF),
            V((*lead, 3, EXP, rows, HID), BF),
        ]

    scratch = [
        V((3, *w_shape), BF), V((4, BLK, PAIR), BF), V((TOK, TOK), BF), V((4, EXP, ROWS, PAIR), BF),
        V((16, PAIR), F32), V((8, TOK), jnp.int32), V((8, TOK), BF),
        *comm(2, ROWS, CAPS), *comm(None, CAPS, NLO),
        V((3, 5, 8, PAIR), F32), V((3, 4, 8, PAIR), F32), V((2, 8, PAIR), F32),
        V((FEAT, PAIR), F32), V((4, CROWS, PAIR), BF), V((4, CROWS, TOK), BF),
        V((4, CROWS, TOK), BF), V((CUT, TOK), BF), V((CROWS - CUT, TOK), BF), V((2, CROWS, TOK), BF),
        pltpu.SemaphoreType.DMA((7,)), pltpu.SemaphoreType.DMA((106,)), pltpu.SemaphoreType.DMA((106,)),
    ]
    gt, gg, ld, og, ou, od = pl.pallas_call(
        kernel,
        name="expert_backward",
        out_shape=(
            V((FEAT, TOK), BF), V((8, TOK), BF), V((1, ALL_EXPERTS), F32),
            V(w_shape, BF), V(w_shape, BF), V(w_shape, BF),
        ),
        in_specs=[any_] * 7,
        out_specs=[pl.BlockSpec(memory_space=pltpu.VMEM)] * 6,
        scratch_shapes=scratch,
        compiler_params=pltpu.CompilerParams(
            collective_id=0, has_side_effects=True, vmem_limit_bytes=54_500_000
        ),
    )(routes.T, gates.T, tokens.T, grad_out.T, w_gate, w_up, jnp.transpose(w_down, (0, 2, 1)))
    return gt.T, gg.T, og, ou, jnp.transpose(od, (0, 2, 1)), ld.reshape(ALL_EXPERTS)


def solution(mesh):
    in_specs = (
        P("node", "local"),
        P("node", "local"),
        P("node", None),
        P("node", None),
        P("node", "local", None),
        P("node", "local", None),
        P("node", None, "local"),
    )
    out_specs = (
        P("node", "local"),
        P("node", None),
        P("node", "local", None),
        P("node", "local", None),
        P("node", None, "local"),
        P(),
    )
    return jax.shard_map(
        on_device, mesh=mesh, in_specs=in_specs, out_specs=out_specs, check_vma=False
    )
```

time: 425 us -> 210 us (0.49)
  waiting for transfers between devices: 228 us -> 0 us
  Pallas kernels: 0 us -> 202 us
  local copies, waits for them, and re-layouts: 70.4 us -> 7.3 us
  matrix products: 55 us -> 0 us
  starting transfers between devices: 30.1 us -> 0 us
  other arithmetic: 25.9 us -> 0 us
  between operations: 14.2 us -> 0.65 us
    pallas_call x0 -> x1, Pallas kernels: none -> 202 us  [on_device(): pl.pallas_call(kernel, name='expert_backward', out_shape=(V((FEAT, TOK),...]
    psum x1 -> x0, waiting for transfers between devices: 180 us -> none  [on_device(): lax.psum(up_pre.astype(jnp.bfloat16), 'local').astype(jnp.float32)]
    dot_general x8 -> x0, matrix products: 55 us -> none  [the longest x1 10.1 us: on_device(): jnp.einsum('sjch,sjcd->jhd', weighted, grad_rows, preferred_element_type=...]
    all_to_all x6 -> x0, waiting for transfers between devices: 48.2 us -> none  [the longest x1 23.4 us: on_device(): lax.all_to_all(send_tokens, 'node', split_axis=0, concat_axis=0, tiled=True)]
    gather x4 -> x0, local copies, waits for them, and re-layouts: 38.6 us -> none  [the longest x1 13.1 us: on_device(): returned_products.reshape(experts * capacity)[target]]
    all_to_all x6 -> x0, starting transfers between devices: 30.1 us -> none  [the longest x1 5.92 us: on_device(): lax.all_to_all(send_tokens, 'node', split_axis=0, concat_axis=0, tiled=True)]
    scatter x2 -> x0, local copies, waits for them, and re-layouts: 22.6 us -> none  [the longest x1 14.6 us: on_device(): jnp.zeros((experts * capacity,), jnp.bfloat16).at[target].set(flat_gates)]
    reduce_sum x5 -> x0, other arithmetic: 15.2 us -> none  [the longest x1 12 us: activation_grads(): products = jnp.sum(hidden * back_hidden, axis=-1)]
  transfers between devices with their start and end apart: 7 -> 0, of which waited for: 4 -> 0; matrix products, arithmetic and copies ran while one was open for 20% -> 0% of each run, Pallas kernels for 0% -> 0%
where the time goes in v2:
time: 210 us
  Pallas kernels  202 us (96%)
  local copies, waits for them, and re-layouts  7.3 us (3%)
    pallas_call x1, Pallas kernels, on_device(): pl.pallas_call(kernel, name='expert_backward', out_shape=(V((FEAT, TOK),...  202 us
    unnamed x6, local copies, waits for them, and re-layouts  7.3 us

profile of v2, /device:TPU:1, one launch (start us, length us, event | category | flops | bytes accessed | tf_op | source)
XLA Modules:
  0.0 209.9 jit_solution(161649148832983019)
XLA Ops:
  0.6 202.0 %expert_backward.1 = (bf16[448,256]{1,0:T(8,128)(2,1)S(1)}, bf16[8,256]{1,0:T(8,128)(2,1)S(1)}, f32[1,32]{1,0:T(1,128)S(1)}, bf16[4,448,1024]{2,1,0:T(8,128)(2,1...) custom-call(s32[8,256]{1,0:T(8,128)} %bitcast.16, bf16[8,256]{1,0:T(8,128)(2,1)} %bitcast.17, ...), custom_call_target="tpu_custom_call" | custom-call | tf_op jit(solution)/shard_map/expert_backward/pallas_call | solution.py:514
  202.6 0.7 copy.19
  203.3 0.6 copy.20
  203.9 0.5 copy.24
  204.4 1.8 copy.21
  206.2 1.8 copy.22
  208.1 1.8 copy.23

commit v3 on v2

--- a/solution.py
+++ b/solution.py
@@ -15,7 +15,7 @@
 HALF = HID // 2
 BLK = 2 * FEAT + 16
 CROWS = FEAT + 16
-CUT = 240
+CUT = 224
 ALL_EXPERTS = 32
 
 
@@ -52,7 +52,7 @@
 def kernel(
     routes_h, gates_h, tok_h, dy_h, wg_h, wu_h, wd_h,
     gt, gg, ld, acc0, acc1, acc2,
-    wt, gat, tri, hot, slot, rbuf, gbuf, prt, r1a, r1b, r2a, r2b, sa, sb, r3a, r3b, r4a, r4b, act,
+    wt, gat, tri, hot, slot, xb, rbuf, gbuf, prt, r1a, r1b, r2a, r2b, sa, sb, r3a, r3b, r4a, r4b, act,
     prt_h, r1a_h, r1b_h, r2a_h, r2b_h, sa_h, sb_h, r3a_h, r3b_h, r4a_h, r4b_h, act_h,
     dv, dr, df, bk, cb, c1r, cs, c2a, c2b, c3r,
     lsem, ssem, rsem,
@@ -105,7 +105,7 @@
     ]
     go(own)
     weights = [pltpu.make_async_copy(h, wt.at[m], lsem.at[4 + m]) for m, h in enumerate((wg_h, wu_h, wd_h))]
-    go(weights)
+    go(weights[:1])
     barrier = pltpu.get_barrier_semaphore()
     for dev in (mate, xpd, xmd, ypd, ymd, zpd, zmd):
         pl.semaphore_signal(barrier, inc=1, device_id=dev, device_id_type=MESH)
@@ -115,6 +115,7 @@
     col_i = lax.broadcasted_iota(jnp.int32, (TOK, TOK), 1)
     tri[...] = jnp.where(row_i < col_i, 1.0, 0.0).astype(BF)
     done(own[2:])
+    go(weights[1:])
     pl.semaphore_wait(barrier, 7)
     first = [
         rc(gat.at[0, :, left], gat.at[0, :, right], 0, mate),
@@ -138,7 +139,7 @@
     k1 = Part(3, (0, ROWS), (0, PAIR), ROWS, CAPS, bufs(1), 20, 1, 1)
     k2 = Part(2, (0, ROWS), (0, PAIR), ROWS, CAPS, bufs(0), 20, 0, 0)
     k3 = Part(1, (0, ROWS), (0, PAIR), ROWS, CAPS, bufs(1), 20, 1, 1)
-    kh = Part(0, (CAPS, ROWS), (TOK, PAIR), CAPS, NLO, half_bufs, 64, 0, 2)
+    kh = Part(0, (CAPS, ROWS), (TOK, PAIR), CAPS, NLO, half_bufs, 80, 0, 2)
 
     def meta_of(k):
         m = gat[k.r, meta_rows, k.ln].astype(F32)
@@ -147,7 +148,7 @@
     def expert_id(e):
         return (node * EXP + e).astype(F32)
 
-    def project(k):
+    def project(k, load=False):
         routes, _ = meta_of(k)
         wide = (16, k.width)
         rid = lax.broadcasted_iota(jnp.int32, wide, 0)
@@ -161,17 +162,32 @@
             slot[:, pl.ds(h * TOK, TOK)] = jnp.where(mine > 0.5, before + float(CAPS * h), -1.0)
         sid = lax.broadcasted_iota(jnp.int32, (k.n, k.width), 0).astype(F32)
 
-        def one_expert(e, carry):
+        def rows_of(e, carry):
             o = jnp.where(sid == slot[pl.ds(e, 1), pl.ds(0, k.width)], 1.0, 0.0).astype(BF)
             hot[k.r, e, k.rw, k.ln] = o
-            xr = dot_t(o, gat[k.r, tok_rows, k.ln]).astype(BF)
-            k.p[0, e, k.all] = dot_n(xr, wt[0, e]).astype(BF)
-            k.p[1, e, k.all] = dot_n(xr, wt[1, e]).astype(BF)
-            gr = dot_t(o, gat[k.r, dy_rows, k.ln]).astype(BF)
-            k.p[2, e, k.all] = dot_n(gr, wt[2, e]).astype(BF)
+            xb[0, e, k.all] = dot_t(o, gat[k.r, tok_rows, k.ln]).astype(BF)
+            xb[1, e, k.all] = dot_t(o, gat[k.r, dy_rows, k.ln]).astype(BF)
             return carry
 
-        lax.fori_loop(0, EXP, one_expert, 0)
+        lax.fori_loop(0, EXP, rows_of, 0)
+
+        if load:
+            for m in range(3):
+                done(weights[m : m + 1])
+
+                def one_product(e, carry):
+                    k.p[m, e, k.all] = dot_n(xb[m // 2, e, k.all], wt[m, e]).astype(BF)
+                    return carry
+
+                lax.fori_loop(0, EXP, one_product, 0)
+        else:
+
+            def products(e, carry):
+                for m in range(3):
+                    k.p[m, e, k.all] = dot_n(xb[m // 2, e, k.all], wt[m, e]).astype(BF)
+                return carry
+
+            lax.fori_loop(0, EXP, products, 0)
 
     def s1(k):
         p, b = k.p, k.base
@@ -190,13 +206,13 @@
             p[m, :, k.lo, lane(zm, HALF)] = add2(p[m, :, k.lo, lane(zm, HALF)], k.r1b[0, m, :, k.nlo])
             p[m, :, k.hi, lane(zp, HALF)] = add2(p[m, :, k.hi, lane(zp, HALF)], k.r1b[1, m, :, k.nhi])
 
-    def s2(k):
-        p, b = k.p, k.base + 4
+    def s2(k, g):
+        p, b, ms = k.p, k.base + 4 + 4 * g, (pl.ds(0, 1), pl.ds(1, 2))[g]
         return [
-            rc(p.at[:, yp, k.all, ca], k.r2a.at[0, :, k.all], b, ypd),
-            rc(p.at[:, ym, k.all, ca], k.r2a.at[1, :, k.all], b + 1, ymd),
-            rc(p.at[:, :, k.all, lane(zp, HALF)], k.r2b.at[0, :, :, k.all], b + 2, zpd),
-            rc(p.at[:, :, k.all, lane(zm, HALF)], k.r2b.at[1, :, :, k.all], b + 3, zmd),
+            rc(p.at[ms, yp, k.all, ca], k.r2a.at[0, ms, k.all], b, ypd),
+            rc(p.at[ms, ym, k.all, ca], k.r2a.at[1, ms, k.all], b + 1, ymd),
+            rc(p.at[ms, :, k.all, lane(zp, HALF)], k.r2b.at[0, ms, :, k.all], b + 2, zpd),
+            rc(p.at[ms, :, k.all, lane(zm, HALF)], k.r2b.at[1, ms, :, k.all], b + 3, zmd),
         ]
 
     def s2_add(k):
@@ -208,7 +224,7 @@
             ).astype(BF)
 
     def s3(k):
-        b = k.base + 8
+        b = k.base + 12
         return [
             rc(k.sa.at[:, k.lo, lane(z2, 0)], k.r3a.at[0, :, k.nlo], b, zmd),
             rc(k.sa.at[:, k.hi, lane(z2, 0)], k.r3a.at[1, :, k.nhi], b + 1, zpd),
@@ -225,7 +241,7 @@
             b[m, yp, k.hi] = add2(b[m, yp, k.hi], k.r3b[1, m, k.nhi])
 
     def s4(k):
-        b = k.base + 12
+        b = k.base + 16
         return [
             rc(k.sa.at[:, k.all, lane(zp, 0)], k.r4a.at[0, :, k.all], b, zpd),
             rc(k.sa.at[:, k.all, lane(zm, 0)], k.r4a.at[1, :, k.all], b + 1, zmd),
@@ -263,30 +279,32 @@
         return rc(dv.at[k.d, step, :, at], dr.at[k.d, step, :, at], b, dev)
 
     def a1(k):
-        t, b = k.t, k.base + 16
+        t, b = k.t, k.base + 20
         az, bz = t.at[:, y, k.all, lane(z, 0)], t.at[:, y, k.all, lane(z, HALF)]
         return [rc(az, az, b, zpd), rc(az, az, b + 1, zmd), rc(bz, bz, b + 2, ypd), rc(bz, bz, b + 3, ymd),
                 share(k, 0, b + 4, d_z1)]
 
     def a2(k):
-        t, b = k.t, k.base + 21
+        t, b = k.t, k.base + 25
         v = [t.at[:, y, k.lo, lane(zm, 0)], t.at[:, y, k.hi, lane(zp, 0)],
              t.at[:, ym, k.lo, lane(z, HALF)], t.at[:, yp, k.hi, lane(z, HALF)]]
         return [rc(v[0], v[0], b, zpd), rc(v[1], v[1], b + 1, zmd), rc(v[2], v[2], b + 2, ypd),
                 rc(v[3], v[3], b + 3, ymd), share(k, 1, b + 4, d_z3)]
 
-    def a3(k):
-        t, b = k.t, k.base + 26
-        ay, bz = t.at[:, y, k.all, ca], t.at[:, :, k.all, lane(z, HALF)]
+    def a3(k, g):
+        t, b, ms = k.t, k.base + 30 + 4 * g, (pl.ds(0, 2), pl.ds(2, 1))[g]
+        ay, bz = t.at[ms, y, k.all, ca], t.at[ms, :, k.all, lane(z, HALF)]
+        own_share = [share(k, 2, b + 4, d_y1)] if g else []
         return [rc(ay, ay, b, ypd), rc(ay, ay, b + 1, ymd), rc(bz, bz, b + 2, zpd), rc(bz, bz, b + 3, zmd),
-                share(k, 2, b + 4, d_y1)]
-
-    def a4(k):
-        t, b = k.t, k.base + 31 + 5 * k.par
-        v = [t.at[:, ym, k.lo, ca], t.at[:, yp, k.hi, ca],
-             t.at[:, :, k.lo, lane(zm, HALF)], t.at[:, :, k.hi, lane(zp, HALF)]]
+                *own_share]
+
+    def a4(k, g):
+        t, b, ms = k.t, k.base + 39 + 9 * k.par + 4 * g, (pl.ds(0, 2), pl.ds(2, 1))[g]
+        v = [t.at[ms, ym, k.lo, ca], t.at[ms, yp, k.hi, ca],
+             t.at[ms, :, k.lo, lane(zm, HALF)], t.at[ms, :, k.hi, lane(zp, HALF)]]
+        own_share = [share(k, 3, b + 4, d_y3)] if g else []
         return [rc(v[0], v[0], b, ypd), rc(v[1], v[1], b + 1, ymd), rc(v[2], v[2], b + 2, zpd),
-                rc(v[3], v[3], b + 3, zmd), share(k, 3, b + 4, d_y3)]
+                rc(v[3], v[3], b + 3, zmd), *own_share]
 
     def dstep(k, step):
         at = pl.ds(0, k.width)
@@ -295,10 +313,12 @@
     def do_s1(k):
         done(s1(k))
         s1_add(k)
-        go(s2(k))
+        go(s2(k, 0))
+        go(s2(k, 1))
 
     def do_s2(k):
-        done(s2(k))
+        done(s2(k, 0))
+        done(s2(k, 1))
         s2_add(k)
         go(s3(k))
 
@@ -315,28 +335,38 @@
     def do_a2(k):
         done(a2(k))
         dstep(k, 1)
-        go(a3(k))
+        go(a3(k, 0))
 
     def do_a3(k):
-        done(a3(k))
+        done(a3(k, 0))
+        done(a3(k, 1))
         dstep(k, 2)
 
-    def post_a(k):
-        done(a4(k))
+    def arrive(k):
+        done(a4(k, 0))
+        done(a4(k, 1))
         dstep(k, 3)
-        at = pl.ds(0, k.width)
-        bk[:, at] = jnp.zeros((FEAT, k.width), F32)
+
+    def post_a(k, start=0, size=FEAT, between=None):
+        at, fr = pl.ds(0, k.width), pl.ds(start, size)
+        bk[fr, at] = jnp.zeros((size, k.width), F32)
 
         def one_expert(e, carry):
-            rb = dot_t(wt[0, e], k.t[0, e, k.all]) + dot_t(wt[1, e], k.t[1, e, k.all])
-            bk[:, at] += dot_n(rb.astype(BF), hot[k.r, e, k.rw, k.ln])
+            rb = dot_t(wt[0, e, fr], k.t[0, e, k.all]) + dot_t(wt[1, e, fr], k.t[1, e, k.all])
+            bk[fr, at] += dot_n(rb.astype(BF), hot[k.r, e, k.rw, k.ln])
             return carry
 
-        lax.fori_loop(0, EXP, one_expert, 0)
-        cb[k.r, tok_rows, k.ln] = bk[:, at].astype(BF)
-        cb[k.r, pl.ds(FEAT, 16), k.ln] = jnp.concatenate(
-            [dv[k.d, 4, :, at], jnp.zeros((8, k.width), F32)], 0
-        ).astype(BF)
+        if between is None:
+            lax.fori_loop(0, EXP, one_expert, 0)
+        else:
+            lax.fori_loop(0, EXP // 2, one_expert, 0)
+            between()
+            lax.fori_loop(EXP // 2, EXP, one_expert, 0)
+        cb[k.r, fr, k.ln] = bk[fr, at].astype(BF)
+        if start + size == FEAT:
+            cb[k.r, pl.ds(FEAT, 16), k.ln] = jnp.concatenate(
+                [dv[k.d, 4, :, at], jnp.zeros((8, k.width), F32)], 0
+            ).astype(BF)
 
     def post_b(k, fresh=False):
         def one_expert(e, carry):
@@ -356,11 +386,36 @@
         done(c1(r))
         cs[r] = add2(cb[r, :, left], c1r[r])
 
-    c2 = [rc(cs.at[2, pl.ds(0, CUT)], c2a, 12, xpd), rc(cs.at[2, pl.ds(CUT, CROWS - CUT)], c2b, 13, xmd)]
-    c3 = [rc(cs.at[1], c3r.at[0], 14, xpd), rc(cs.at[3], c3r.at[1], 15, xmd)]
-
-    done(weights)
-    project(k0)
+    top, low = pl.ds(0, CUT), pl.ds(CUT, CROWS - CUT)
+    c2 = [rc(cs.at[2, top], c2a, 12, xpd), rc(cs.at[2, low], c2b, 13, xmd)]
+    c1_last = [rc(cb.at[1, top, right], c1r.at[1, top], 9, mate), rc(cb.at[1, low, right], c1r.at[1, low], 16, mate)]
+    c3 = [
+        rc(cs.at[1, top], c3r.at[0, top], 14, xpd),
+        rc(cs.at[1, low], c3r.at[0, low], 17, xpd),
+        rc(cs.at[3], c3r.at[1], 15, xmd),
+    ]
+
+    def count_loads():
+        eid = lax.broadcasted_iota(jnp.int32, (1, ALL_EXPERTS), 1)
+        ld[...] = jnp.zeros_like(ld)
+
+        def one_block(b, carry):
+            r = (b // 2 - x + 4) % 4
+            cc = (b % 2 + c) % 2
+            m = gat[r, meta_rows, pl.ds(pl.multiple_of(cc * TOK, TOK), TOK)].astype(F32)
+            routes, gates = m[:8], m[8:]
+            tot = jnp.zeros((1, ALL_EXPERTS), F32)
+            for e in range(ALL_EXPERTS):
+                v = jnp.sum(jnp.where(routes == float(e), gates, 0.0), axis=0, keepdims=True)
+                v = jnp.sum(v, axis=1, keepdims=True)
+                tot = jnp.where(eid == e, jnp.broadcast_to(v, (1, ALL_EXPERTS)), tot)
+            ld[...] += tot
+            return carry
+
+        lax.fori_loop(0, 8, one_block, 0)
+        ld[...] = ld[...] * (1.0 / 64.0)
+
+    project(k0, True)
     go(s1(k0))
     done(first[:1])
     project(kh)
@@ -375,114 +430,142 @@
     go(s1(k1))
     do_s2(kh)
     do_s3(k0)
-    do_s3(kh)
+    done(second[:2])
+    done(second[3:])
+    go(third)
+    done(s1(k1))
+    s1_add(k1)
+    go(s2(k1, 0))
     done(s4(k0))
     activate(k0)
     go(a1(k0))
-    do_s1(k1)
+    do_s3(kh)
+    go(s2(k1, 1))
+
+    done(third)
+    count_loads()
+    project(k2)
+    do_a1(k0)
     done(s4(kh))
     activate(kh)
-    do_a1(k0)
-    done(second[:2])
-    done(second[3:])
-    go(third)
+    go(a1(kh))
+    do_s2(k1)
     do_a2(k0)
-
-    done(third)
-    project(k2)
-    do_s2(k1)
-    do_a3(k0)
+    go(a3(k0, 1))
     do_s3(k1)
     go(s1(k2))
-    go(a4(k0))
     done(s4(k1))
     activate(k1)
     go(a1(k1))
 
     done(s1(k2))
     s1_add(k2)
+    go(s2(k2, 0))
+    do_a3(k0)
+    go(a4(k0, 0))
+    go(a4(k0, 1))
     do_a1(k1)
-    go(s2(k2))
+    go(s2(k2, 1))
     do_a2(k1)
+    arrive(k0)
     post_a(k0)
     post_b(k0, True)
+    do_s2(k2)
+    go(a3(k1, 1))
     project(k3)
-    do_s2(k2)
-    do_a3(k1)
     do_s3(k2)
     go(s1(k3))
-    go(a4(k1))
+    do_a3(k1)
+    go(a4(k1, 0))
+    go(a4(k1, 1))
+    do_a1(kh)
     done(s4(k2))
     activate(k2)
     go(a1(k2))
 
     done(s1(k3))
     s1_add(k3)
+    go(s2(k3, 0))
     do_a1(k2)
-    go(s2(k3))
+    go(s2(k3, 1))
     do_a2(k2)
+    arrive(k1)
     post_a(k1)
     go(c1(3))
     post_b(k1)
     do_s2(k3)
+    go(a3(k2, 1))
+    do_s3(k3)
     do_a3(k2)
-    do_s3(k3)
-    go(a4(k2))
+    go(a4(k2, 0))
+    go(a4(k2, 1))
     done(s4(k3))
     activate(k3)
     go(a1(k3))
 
+    do_a2(kh)
+    go(a3(kh, 1))
     do_c1(3)
     do_a1(k3)
+    do_a3(kh)
+    go(a4(kh, 0))
+    go(a4(kh, 1))
     do_a2(k3)
-    go(a1(kh))
+    go(a3(k3, 1))
+    arrive(k2)
     post_a(k2)
     go(c1(2))
     post_b(k2)
     do_c1(2)
     go(c2)
-    do_a3(k3)
-    go(a4(k3))
-    do_a1(kh)
-    done(c2)
-    cs[3, pl.ds(CUT, CROWS - CUT), :] = add2(cs[3, pl.ds(CUT, CROWS - CUT), :], c2b[...])
-    c3[1].start()
-    do_a2(kh)
-    post_a(k3)
-    go(c1(1))
-    do_c1(1)
-    cs[1, pl.ds(0, CUT), :] = add2(cs[1, pl.ds(0, CUT), :], c2a[...])
-    c3[0].start()
-    do_a3(kh)
-    go(a4(kh))
-    post_b(k3)
+    done(a3(k3, 0))
+    go(a4(k3, 0))
+    arrive(kh)
     post_a(kh)
     go(c1(0))
+    done(a3(k3, 1))
+    dstep(k3, 2)
+    go(a4(k3, 1))
+    done(c2)
+    cs[3, low, :] = add2(cs[3, low, :], c2b[...])
+    c3[2].start()
     post_b(kh)
-
-    eid = lax.broadcasted_iota(jnp.int32, (1, ALL_EXPERTS), 1)
-    ld[...] = jnp.zeros_like(ld)
-
-    def one_block(b, carry):
-        r = (b // 2 - x + 4) % 4
-        cc = (b % 2 + c) % 2
-        m = gat[r, meta_rows, pl.ds(pl.multiple_of(cc * TOK, TOK), TOK)].astype(F32)
-        routes, gates = m[:8], m[8:]
-        tot = jnp.zeros((1, ALL_EXPERTS), F32)
-        for e in range(ALL_EXPERTS):
-            s = jnp.sum(jnp.where(routes == float(e), gates, 0.0), axis=0, keepdims=True)
-            s = jnp.sum(s, axis=1, keepdims=True)
-            tot = jnp.where(eid == e, jnp.broadcast_to(s, (1, ALL_EXPERTS)), tot)
-        ld[...] += tot
-        return carry
-
-    lax.fori_loop(0, 8, one_block, 0)
-    ld[...] = ld[...] * (1.0 / 64.0)
     do_c1(0)
-    done(c3)
-    total = add3(cs[0], c3r[0], c3r[1])
-    gt[...] = total[:FEAT].astype(BF)
-    gg[...] = total[FEAT : FEAT + 8].astype(BF)
+    done(a4(k3, 0))
+    post_a(k3, 0, CUT)
+    c1_last[0].start()
+    done(a4(k3, 1))
+    dstep(k3, 3)
+
+    def send_top():
+        c1_last[0].wait()
+        cs[1, top, :] = add3(cb[1, top, left], c1r[1, top], c2a[...]).astype(BF)
+        c3[0].start()
+
+    post_a(k3, CUT, FEAT - CUT, send_top)
+    c1_last[1].start()
+    c1_last[1].wait()
+    cs[1, low, :] = add2(cb[1, low, left], c1r[1, low])
+    c3[1].start()
+    post_b(k3)
+    c3[2].wait()
+    c3[0].wait()
+    gt[top, :] = add3(cs[0, top], c3r[0, top], c3r[1, top]).astype(BF)
+    c3[1].wait()
+    rest = add3(cs[0, low], c3r[0, low], c3r[1, low])
+    gt[pl.ds(CUT, FEAT - CUT), :] = rest[: FEAT - CUT].astype(BF)
+    gg[...] = rest[FEAT - CUT : FEAT - CUT + 8].astype(BF)
+
+
+def flush(g0, g1, g2, g3, g4, g5, o0, o1, o2, o3, o4, o5, sem):
+    copies = [
+        pltpu.make_async_copy(a, b, sem.at[n])
+        for n, (a, b) in enumerate(((g3, o3), (g4, o4), (g5, o5), (g0, o0), (g1, o1), (g2, o2)))
+    ]
+    for cp in copies:
+        cp.start()
+    for cp in copies:
+        cp.wait()
 
 
 def on_device(tokens, grad_out, gates, routes, w_gate, w_up, w_down):
@@ -504,14 +587,14 @@
 
     scratch = [
         V((3, *w_shape), BF), V((4, BLK, PAIR), BF), V((TOK, TOK), BF), V((4, EXP, ROWS, PAIR), BF),
-        V((16, PAIR), F32), V((8, TOK), jnp.int32), V((8, TOK), BF),
+        V((16, PAIR), F32), V((2, EXP, ROWS, FEAT), BF), V((8, TOK), jnp.int32), V((8, TOK), BF),
         *comm(2, ROWS, CAPS), *comm(None, CAPS, NLO),
         V((3, 5, 8, PAIR), F32), V((3, 4, 8, PAIR), F32), V((2, 8, PAIR), F32),
         V((FEAT, PAIR), F32), V((4, CROWS, PAIR), BF), V((4, CROWS, TOK), BF),
         V((4, CROWS, TOK), BF), V((CUT, TOK), BF), V((CROWS - CUT, TOK), BF), V((2, CROWS, TOK), BF),
-        pltpu.SemaphoreType.DMA((7,)), pltpu.SemaphoreType.DMA((106,)), pltpu.SemaphoreType.DMA((106,)),
+        pltpu.SemaphoreType.DMA((7,)), pltpu.SemaphoreType.DMA((128,)), pltpu.SemaphoreType.DMA((128,)),
     ]
-    gt, gg, ld, og, ou, od = pl.pallas_call(
+    results = pl.pallas_call(
         kernel,
         name="expert_backward",
         out_shape=(
@@ -522,9 +605,22 @@
         out_specs=[pl.BlockSpec(memory_space=pltpu.VMEM)] * 6,
         scratch_shapes=scratch,
         compiler_params=pltpu.CompilerParams(
-            collective_id=0, has_side_effects=True, vmem_limit_bytes=54_500_000
+            collective_id=0, has_side_effects=True, vmem_limit_bytes=54_000_000
         ),
     )(routes.T, gates.T, tokens.T, grad_out.T, w_gate, w_up, jnp.transpose(w_down, (0, 2, 1)))
+    shape = jax.ShapeDtypeStruct
+    gt, gg, ld, og, ou, od = pl.pallas_call(
+        flush,
+        name="write_results",
+        out_shape=(
+            shape((FEAT, TOK), BF), shape((8, TOK), BF), shape((1, ALL_EXPERTS), F32),
+            shape(w_shape, BF), shape(w_shape, BF), shape(w_shape, BF),
+        ),
+        in_specs=[pl.BlockSpec(memory_space=pltpu.VMEM)] * 6,
+        out_specs=[any_] * 6,
+        scratch_shapes=[pltpu.SemaphoreType.DMA((6,))],
+        compiler_params=pltpu.CompilerParams(vmem_limit_bytes=8_000_000),
+    )(*results)
     return gt.T, gg.T, og, ou, jnp.transpose(od, (0, 2, 1)), ld.reshape(ALL_EXPERTS)
 
 

time: 210 us -> 198 us (0.943)
  local copies, waits for them, and re-layouts: 7.3 us -> 0 us
  Pallas kernels: 202 us -> 197 us
    pallas_call x1, Pallas kernels: 202 us -> 192 us  [on_device(): pl.pallas_call(kernel, name='expert_backward', out_shape=(V((FEAT, TOK),...]
    unnamed x6 -> x0, local copies, waits for them, and re-layouts: 7.3 us -> none
    pallas_call x0 -> x1, Pallas kernels: none -> 4.31 us  [on_device(): pl.pallas_call(flush, name='write_results', out_shape=(shape((FEAT, TOK),...]
where the time goes in v3:
time: 198 us; the launch traced here: 197 us
  Pallas kernels  197 us (99%)
    pallas_call x1, Pallas kernels, on_device(): pl.pallas_call(kernel, name='expert_backward', out_shape=(V((FEAT, TOK),...  192 us
    pallas_call x1, Pallas kernels, on_device(): pl.pallas_call(flush, name='write_results', out_shape=(shape((FEAT, TOK),...  4.31 us

profile of v3, /device:TPU:1, one launch (start us, length us, event | category | flops | bytes accessed | tf_op | source)
XLA Modules:
  0.0 197.5 jit_solution(5266336471665498727)
XLA Ops:
  0.6 192.4 %expert_backward.1 = (bf16[448,256]{1,0:T(8,128)(2,1)S(1)}, bf16[8,256]{1,0:T(8,128)(2,1)S(1)}, f32[1,32]{1,0:T(1,128)S(1)}, bf16[4,448,1024]{2,1,0:T(8,128)(2,1...) custom-call(s32[8,256]{1,0:T(8,128)} %bitcast.12, bf16[8,256]{1,0:T(8,128)(2,1)} %bitcast.13, ...), custom_call_target="tpu_custom_call" | custom-call | tf_op jit(solution)/shard_map/expert_backward/pallas_call | solution.py:597
  193.0 4.3 %write_results.1 = (bf16[448,256]{1,0:T(8,128)(2,1)}, bf16[8,256]{1,0:T(8,128)(2,1)}, f32[1,32]{1,0:T(1,128)}, bf16[4,448,1024]{2,1,0:T(8,128)(2,1)}, bf16[4,448...) custom-call(bf16[448,256]{1,0:T(8,128)(2,1)S(1)} %get-tuple-element.18.g0, bf16[8,256]{1,0:T(8,128)(2,1)S(1)} %get-tuple-element.19.g1, ...), custom_call_target="tpu_custom_call" | custom-call | tf_op jit(solution)/shard_map/write_results/pallas_call | solution.py:612

commit v4 on v3

--- a/solution.py
+++ b/solution.py
@@ -52,7 +52,7 @@
 def kernel(
     routes_h, gates_h, tok_h, dy_h, wg_h, wu_h, wd_h,
     gt, gg, ld, acc0, acc1, acc2,
-    wt, gat, tri, hot, slot, xb, rbuf, gbuf, prt, r1a, r1b, r2a, r2b, sa, sb, r3a, r3b, r4a, r4b, act,
+    wt, gat, tri, hot, slot, xb, tb, rbuf, gbuf, prt, r1a, r1b, r2a, r2b, sa, sb, r3a, r3b, r4a, r4b, act,
     prt_h, r1a_h, r1b_h, r2a_h, r2b_h, sa_h, sb_h, r3a_h, r3b_h, r4a_h, r4b_h, act_h,
     dv, dr, df, bk, cb, c1r, cs, c2a, c2b, c3r,
     lsem, ssem, rsem,
@@ -148,7 +148,7 @@
     def expert_id(e):
         return (node * EXP + e).astype(F32)
 
-    def project(k, load=False):
+    def slot_rows(k):
         routes, _ = meta_of(k)
         wide = (16, k.width)
         rid = lax.broadcasted_iota(jnp.int32, wide, 0)
@@ -165,29 +165,55 @@
         def rows_of(e, carry):
             o = jnp.where(sid == slot[pl.ds(e, 1), pl.ds(0, k.width)], 1.0, 0.0).astype(BF)
             hot[k.r, e, k.rw, k.ln] = o
-            xb[0, e, k.all] = dot_t(o, gat[k.r, tok_rows, k.ln]).astype(BF)
-            xb[1, e, k.all] = dot_t(o, gat[k.r, dy_rows, k.ln]).astype(BF)
+            xb[0, e, k.rw] = dot_t(o, gat[k.r, tok_rows, k.ln]).astype(BF)
+            xb[1, e, k.rw] = dot_t(o, gat[k.r, dy_rows, k.ln]).astype(BF)
             return carry
 
         lax.fori_loop(0, EXP, rows_of, 0)
 
-        if load:
+    def project(k):
+        slot_rows(k)
+
+        def products(e, carry):
             for m in range(3):
-                done(weights[m : m + 1])
-
-                def one_product(e, carry):
-                    k.p[m, e, k.all] = dot_n(xb[m // 2, e, k.all], wt[m, e]).astype(BF)
-                    return carry
-
-                lax.fori_loop(0, EXP, one_product, 0)
-        else:
-
-            def products(e, carry):
-                for m in range(3):
-                    k.p[m, e, k.all] = dot_n(xb[m // 2, e, k.all], wt[m, e]).astype(BF)
-                return carry
-
-            lax.fori_loop(0, EXP, products, 0)
+                k.p[m, e, k.all] = dot_n(xb[m // 2, e, k.rw], wt[m, e]).astype(BF)
+            return carry
+
+        lax.fori_loop(0, EXP, products, 0)
+
+    def half_product(k):
+        def one_half(j, carry):
+            e = (y2 + j) % 4
+            for m in range(3):
+                k.p[m, e, k.all, ca] = dot_n(xb[m // 2, e, k.rw], wt[m, e, :, ca]).astype(BF)
+            return carry
+
+        return one_half
+
+    def first_products(k):
+        at = lane(z2, HALF)
+        lax.fori_loop(0, 1, half_product(k), 0)
+
+        def one_column(e, carry):
+            for m in range(3):
+                k.p[m, e, k.all, at] = dot_n(xb[m // 2, e, k.rw], wt[m, e, :, at]).astype(BF)
+            return carry
+
+        lax.fori_loop(0, EXP, one_column, 0)
+
+    def rest_products(k):
+        lax.fori_loop(1, EXP, half_product(k), 0)
+
+        def other_columns(e, carry):
+            for m in range(3):
+                tb[m, k.all] = dot_n(xb[m // 2, e, k.rw], wt[m, e, :, pl.ds(HALF, HALF)]).astype(BF)
+            for m in range(3):
+                for j in range(1, 4):
+                    q = (z2 + j) % 4
+                    k.p[m, e, k.all, lane(q, HALF)] = tb[m, k.all, lane(q, 0)]
+            return carry
+
+        lax.fori_loop(0, EXP, other_columns, 0)
 
     def s1(k):
         p, b = k.p, k.base
@@ -415,15 +441,20 @@
         lax.fori_loop(0, 8, one_block, 0)
         ld[...] = ld[...] * (1.0 / 64.0)
 
-    project(k0, True)
+    slot_rows(k0)
+    done(weights)
+    first_products(k0)
     go(s1(k0))
     done(first[:1])
-    project(kh)
+    slot_rows(kh)
+    first_products(kh)
     go(s1(kh))
+    rest_products(k0)
     do_s1(k0)
-    do_s1(kh)
+    rest_products(kh)
     done(first[1:])
     go(second)
+    do_s1(kh)
     done(second[2:3])
     project(k1)
     do_s2(k0)
@@ -476,12 +507,12 @@
     do_s3(k2)
     go(s1(k3))
     do_a3(k1)
-    go(a4(k1, 0))
-    go(a4(k1, 1))
     do_a1(kh)
     done(s4(k2))
     activate(k2)
     go(a1(k2))
+    go(a4(k1, 0))
+    go(a4(k1, 1))
 
     done(s1(k3))
     s1_add(k3)
@@ -587,7 +618,8 @@
 
     scratch = [
         V((3, *w_shape), BF), V((4, BLK, PAIR), BF), V((TOK, TOK), BF), V((4, EXP, ROWS, PAIR), BF),
-        V((16, PAIR), F32), V((2, EXP, ROWS, FEAT), BF), V((8, TOK), jnp.int32), V((8, TOK), BF),
+        V((16, PAIR), F32), V((2, EXP, ROWS, FEAT), BF), V((3, CAPS, HALF), BF),
+        V((8, TOK), jnp.int32), V((8, TOK), BF),
         *comm(2, ROWS, CAPS), *comm(None, CAPS, NLO),
         V((3, 5, 8, PAIR), F32), V((3, 4, 8, PAIR), F32), V((2, 8, PAIR), F32),
         V((FEAT, PAIR), F32), V((4, CROWS, PAIR), BF), V((4, CROWS, TOK), BF),
@@ -605,7 +637,7 @@
         out_specs=[pl.BlockSpec(memory_space=pltpu.VMEM)] * 6,
         scratch_shapes=scratch,
         compiler_params=pltpu.CompilerParams(
-            collective_id=0, has_side_effects=True, vmem_limit_bytes=54_000_000
+            collective_id=0, has_side_effects=True, vmem_limit_bytes=54_400_000
         ),
     )(routes.T, gates.T, tokens.T, grad_out.T, w_gate, w_up, jnp.transpose(w_down, (0, 2, 1)))
     shape = jax.ShapeDtypeStruct

time: 198 us -> 196 us (0.990)
  Pallas kernels: 197 us -> 195 us
where the time goes in v4:
time: 196 us
  Pallas kernels  195 us (99%)
    pallas_call x1, Pallas kernels, on_device(): pl.pallas_call(kernel, name='expert_backward', out_shape=(V((FEAT, TOK),...  191 us
    pallas_call x1, Pallas kernels, on_device(): pl.pallas_call(flush, name='write_results', out_shape=(shape((FEAT, TOK),...  4.31 us

profile of v4, /device:TPU:1, one launch (start us, length us, event | category | flops | bytes accessed | tf_op | source)
XLA Modules:
  0.0 195.8 jit_solution(6923328616214158660)
XLA Ops:
  0.6 190.7 %expert_backward.1 = (bf16[448,256]{1,0:T(8,128)(2,1)S(1)}, bf16[8,256]{1,0:T(8,128)(2,1)S(1)}, f32[1,32]{1,0:T(1,128)S(1)}, bf16[4,448,1024]{2,1,0:T(8,128)(2,1...) custom-call(s32[8,256]{1,0:T(8,128)} %bitcast.12, bf16[8,256]{1,0:T(8,128)(2,1)} %bitcast.13, ...), custom_call_target="tpu_custom_call" | custom-call | tf_op jit(solution)/shard_map/expert_backward/pallas_call | solution.py:629
  191.3 4.3 %write_results.1 = (bf16[448,256]{1,0:T(8,128)(2,1)}, bf16[8,256]{1,0:T(8,128)(2,1)}, f32[1,32]{1,0:T(1,128)}, bf16[4,448,1024]{2,1,0:T(8,128)(2,1)}, bf16[4,448...) custom-call(bf16[448,256]{1,0:T(8,128)(2,1)S(1)} %get-tuple-element.18.g0, bf16[8,256]{1,0:T(8,128)(2,1)S(1)} %get-tuple-element.19.g1, ...), custom_call_target="tpu_custom_call" | custom-call | tf_op jit(solution)/shard_map/write_results/pallas_call | solution.py:644
